TPU v7x, 256 devices: a whole 4x4x8 slice. The times are simulated.
256 devices in a mesh: sx: 16 (over y, z_lo), sy: 16 (over z_hi, x, core).
Axes of the slice: x: 4, y: 4, z: 8 (z_hi: 2, z_lo: 4; z = z_hi * 4 + z_lo), core: 2. Of those that a mesh axis runs over, the one named last changes fastest.
Arguments:
- schur: float32 [16, 16, 1024, 1024], P('sx', 'sy'), may hold values from -60 to 300, as said below
- rhs_local: float32 [16, 16, 1024], P('sx', 'sy'), may hold values from -1 to 10
- edge_perm: int32 [16, 16, 4, 2], P('sx', 'sy'), may hold values from 0 to 1, each once within a row
- chol_interior: float32 [16, 16, 512, 512], P('sx', 'sy'), may hold values from -1 to 2, as said below
- coupling: bfloat16 [16, 16, 512, 1024], P('sx', 'sy'), may hold values from -0.25 to 0.25
- boundary_diag: float32 [16, 16, 1024], P('sx', 'sy'), may hold values from 1 to 3
- restrict: bfloat16 [16, 16, 768, 1024], P('sx', 'sy'), may hold values from -0.1875 to 0.1875
- extend: bfloat16 [16, 16, 1024, 768], P('sx', 'sy'), may hold values from -0.1875 to 0.1875
Outputs:
- solution: float32 [16, 16, 1024], P('sx', 'sy')
- residual: float32 [16, 16, 1024], P('sx', 'sy')
- schur_next: bfloat16 [16, 16, 1024, 1024], P('sx', 'sy')
- coarse: float32 [768, 768], P('sx', 'sy')
Inputs may be any that keep to these rules, and one draw needn't show every extreme that they name: `schur`: each subdomain's matrix is symmetric positive definite; its scale differs from subdomain to subdomain. `chol_interior`: lower triangular with diagonal between 1 and 2.
All inputs are finite; a program needn't handle non-finite values.
Results may differ from a plain program's by a relative error of at most 0.0055.
Values sent between devices are 32-bit elements; how exact they have to be, the bound alone decides.
A program may use at most 64 MiB of HBM per device.

v0:
```python
import functools

import jax
import jax.numpy as jnp
from jax import lax
from jax.sharding import Mesh
from jax.sharding import PartitionSpec as P

NB = 1024
BLK = 128
ITERS = 3
EB = 2
SX_SY = ("sx_0", "sx_1", "sy_0", "sy_1", "sy_2")
SX = ("sx_0", "sx_1")
SY = ("sy_0", "sy_1", "sy_2")


def padded_2(x, sides, width):
    edges = {}
    for axis, dim in sides:
        peers, length = (lax.axis_size(axis), x.shape[dim])
        up = [(i, (i + 1) % peers) for i in range(peers)]
        last = lax.slice_in_dim(x, length - width, length, axis=dim)
        leading = lax.slice_in_dim(x, 0, width, axis=dim)
        edges[dim] = (
            lax.ppermute(last, axis, up),
            lax.ppermute(leading, axis, [(b, a) for a, b in up]),
        )
    done = []
    for _, dim in sides:
        low, high = edges[dim]
        around = [(width, width) if d in done else (0, 0) for d in range(x.ndim)]
        x = jnp.concatenate([jnp.pad(low, around), x, jnp.pad(high, around)], axis=dim)
        done.append(dim)
    return x


def by_axis(x, axes):
    return functools.reduce(lax.psum, axes, x)


def cut_along(x, dim, peers):
    shape = x.shape
    tiles = x.reshape(*shape[:dim], peers, shape[dim] // peers, *shape[dim + 1 :])
    return jnp.moveaxis(tiles, dim, 0)


def summed_on_arrival(x, axis, dim):
    peers = lax.axis_size(axis)
    tiles = lax.all_to_all(cut_along(x, dim, peers), axis, 0, 0, tiled=True)
    return jnp.sum(tiles, axis=0)


def assemble(vectors, perm_hot):
    members = vectors.shape[0]
    blocks = vectors.reshape(members, 4, EB, BLK)
    canonical = jnp.einsum(
        "dkc,mdkf->dcmf", perm_hot, blocks, precision=lax.Precision.HIGHEST
    ).reshape(4, EB, members * BLK)
    face_grid = jnp.zeros((EB + 2, EB + 2, members * BLK), jnp.float32)
    face_grid = (
        face_grid.at[0, 1 : EB + 1].set(canonical[2]).at[EB + 1, 1 : EB + 1].set(canonical[3])
    )
    face_grid = (
        face_grid.at[1 : EB + 1, 0].set(canonical[0]).at[1 : EB + 1, EB + 1].set(canonical[1])
    )
    padded = padded_2(face_grid, ((SX, 0), (SY, 1)), 1)
    received = jnp.stack(
        [
            padded[2 : EB + 2, 0],
            padded[2 : EB + 2, EB + 3],
            padded[0, 2 : EB + 2],
            padded[EB + 3, 2 : EB + 2],
        ]
    )
    received = received.reshape(4, EB, members, BLK)
    mapped = jnp.einsum(
        "dkc,dcmf->mdkf", perm_hot, received, precision=lax.Precision.HIGHEST
    ).reshape(members, NB)
    return vectors + mapped


def paired_sums(residual, scaled, image):
    return (
        by_axis(0.5 * jnp.sum(residual * scaled), SX_SY),
        by_axis(0.5 * jnp.sum(scaled * image), SX_SY),
    )


def per_device(
    schur, rhs_local, edge_perm, chol_interior, coupling, boundary_diag, restrict, extend
):
    local_schur = schur[0, 0]
    block_order = edge_perm[0, 0]
    perm_hot = (block_order[:, :, None] == jnp.arange(EB, dtype=jnp.int32)[None, None, :]).astype(
        jnp.float32
    )
    assembled = assemble(jnp.stack([rhs_local[0, 0], jnp.diagonal(local_schur)]), perm_hot)
    right_side = assembled[0]
    precond = assembled[1]

    def operator(field):
        product = jnp.dot(local_schur, field, precision=lax.Precision.HIGHEST)
        return assemble(product[None, :], perm_hot)[0]

    solution = jnp.zeros_like(right_side)
    residual = right_side
    scaled = residual / precond
    image = operator(scaled)
    norm_now, curvature = paired_sums(residual, scaled, image)
    step_size = norm_now / curvature
    direction = scaled
    along = image
    for step in range(ITERS):
        solution = solution + step_size * direction
        residual = residual - step_size * along
        if step + 1 < ITERS:
            scaled = residual / precond
            image = operator(scaled)
            norm_next, curvature = paired_sums(residual, scaled, image)
            ratio = norm_next / norm_now
            step_size = norm_next / (curvature - ratio * norm_next / step_size)
            direction = scaled + ratio * direction
            along = image + ratio * along
            norm_now = norm_next
    solved = lax.linalg.triangular_solve(
        chol_interior[0, 0], coupling[0, 0].astype(jnp.float32), left_side=True, lower=True
    )
    interior = solved.astype(jnp.bfloat16)
    gram = lax.dot_general(
        interior, interior, (((0,), (0,)), ((), ())), preferred_element_type=jnp.float32
    )
    following = (jnp.diag(boundary_diag[0, 0]) - gram).astype(jnp.bfloat16)
    projected = jnp.dot(following, extend[0, 0], preferred_element_type=jnp.float32).astype(
        jnp.bfloat16
    )
    restrict_rows = restrict[0, 0]
    row_block = lax.psum_scatter(
        jnp.dot(restrict_rows, projected, preferred_element_type=jnp.float32),
        SX,
        scatter_dimension=0,
        tiled=True,
    )
    coarse = summed_on_arrival(row_block, SY, 1)
    return (solution[None, None], residual[None, None], following[None, None], coarse)


def solution(mesh):
    finer = Mesh(mesh.devices.reshape(4, 4, 2, 4, 2), ("sx_0", "sx_1", "sy_0", "sy_1", "sy_2"))
    return jax.shard_map(
        per_device,
        mesh=finer,
        in_specs=(
            P(SX, SY, None, None),
            P(SX, SY, None),
            P(SX, SY, None, None),
            P(SX, SY, None, None),
            P(SX, SY, None, None),
            P(SX, SY, None),
            P(SX, SY, None, None),
            P(SX, SY, None, None),
        ),
        out_specs=(P(SX, SY, None), P(SX, SY, None), P(SX, SY, None, None), P(SX, SY)),
        check_vma=False,
    )
```

profile of v0, /device:TPU:1, one launch (start us, length us, event | category | flops | bytes accessed | tf_op | source)
XLA Modules:
  0.0 351.6 jit_solution(4157814219036144333)
XLA Ops:
  8.1 17.4 %gather_fusion = f32[1024]{0:T(1024)S(1)} fusion(f32[1024,1024]{1,0:T(8,128)} %bitcast.180, s32[1024]{0:T(1024)S(1)} %bitcast.179), kind=kCustom, calls=%fused_computation | custom fusion | bytes 16384 | tf_op jit(solution)/shard_map/jit(diagonal)/cond/branch_0_fun/gather | solution.py:98
  28.1 2.7 collective-permute-start
  31.5 6.1 %collective-permute-start.3 = (f32[1,4,256]{2,1,0:T(4,128)S(1)}, f32[1,4,256]{2,1,0:T(4,128)S(1)}, u32[]{:S(2)}, u32[]{:S(2)}) collective-permute-start(f32[1,4,256]{2,1,0:T(4,128)S(1)} %get-tuple-element.265), channel_id=1, source_target_pairs={{16,0},{32,16},{48,32},{64,48},{80,64},{96,80},{112,96},{128,112},... | collective-permute-start | bytes 12296 | tf_op jit(solution)/shard_map/ppermute | solution.py:27
  39.1 8.5 %while.17 = (s32[]{:T(128)}, f32[512,512]{1,0:T(8,128)S(1)}, s32[4,2]{0,1:T(2,128)S(1)}, f32[4,128,128]{2,1,0:T(8,128)S(1)}, s32[]{:T(128)}) while((s32[]{:T(128)}, f32[512,512]{1,0:T(8,128)S(1)}, s32[4,2]{0,1:T(2,128)S(1)}, f32[4,128,128]{2,1,0:T(8,128)S(1)}, s32[]{:T(128)}) %tuple.124), condition=%wide.while_cond.16, body=%wide.while_body.16.sunk | while | flops 2 | bytes 131181 | solution.py:126
  47.6 39.3 %custom-call.3 = f32[4,128,128]{1,2,0:T(8,128)S(1)} custom-call(f32[4,128,128]{2,1,0:T(8,128)S(1)} %get-tuple-element.203), custom_call_target="InvertDiagBlocksLowerTriangular" | custom-call | tf_op jit(solution)/shard_map/triangular_solve | solution.py:126
  94.1 2.6 subtract_convert_fusion
  96.7 7.1 %convolution_bitcast_fusion = f32[768,768]{0,1:T(8,128)} fusion(bf16[1,1,768,1024]{3,2,1,0:T(8,128)(2,1)S(1)} %copy-done, bf16[1024,1024]{1,0:T(8,128)(2,1)} %subtract_convert_fusion, bf16[1,1,1024,768]{3,2,1,0:T(8,128)(2,1)} %param.47), kind=kOutput, calls=%fused_computation.5 | convolution fusion | flops 2819358720 | bytes 7602176 | tf_op jit(solution)/shard_map/dot_general | solution.py:139
  103.8 3.3 copy.63
  107.5 5.7 %fusion.43 = f32[1,1024]{1,0:T(1,128)S(1)} fusion(f32[1,1,1024,1024]{3,2,1,0:T(8,128)} %param.40, f32[2,1024]{1,0:T(2,128)S(1)} %maximum_add_fusion), kind=kOutput, calls=%fused_computation.65 | convolution fusion | flops 12583936 | bytes 4206592 | tf_op jit(solution)/shard_map/dot_general | solution.py:103
  117.2 5.0 %collective-permute-start.5 = (f32[4,1,128]{2,1,0:T(1,128)S(1)}, f32[4,1,128]{2,1,0:T(1,128)S(1)}, u32[]{:S(2)}, u32[]{:S(2)}) collective-permute-start(f32[4,1,128]{2,1,0:T(1,128)S(1)} %get-tuple-element.275), channel_id=1, source_target_pairs={{1,0},{2,1},{3,2},{4,3},{5,4},{6,5},{7,6},{8,7},{9,8},{10,9},{11,1... | collective-permute-start | bytes 6152 | tf_op jit(solution)/shard_map/ppermute | solution.py:27
  122.2 5.6 %collective-permute-start.7 = (f32[1,4,128]{2,1,0:T(4,128)S(1)}, f32[1,4,128]{2,1,0:T(4,128)S(1)}, u32[]{:S(2)}, u32[]{:S(2)}) collective-permute-start(f32[1,4,128]{2,1,0:T(4,128)S(1)} %get-tuple-element.277), channel_id=1, source_target_pairs={{16,0},{32,16},{48,32},{64,48},{80,64},{96,80},{112,96},{128,112},... | collective-permute-start | bytes 6152 | tf_op jit(solution)/shard_map/ppermute | solution.py:27
  131.1 6.6 %all-reduce.8 = (f32[]{:T(128)}, f32[]{:T(128)}) all-reduce(f32[]{:T(128)S(6)} %mul.127, f32[]{:T(128)S(6)} %mul.129), channel_id=1, replica_groups=mesh['sx_0'=4,'sx_1'=4,'sy_0'=2,'sy_1'=4,'sy_2'=2] {'sx_0'}, use_global_device_ids=true, to_apply=%region_1.2 | all-reduce | flops 2 | bytes 16 | tf_op jit(solution)/shard_map/psum | solution.py:39
  137.7 13.8 %all-reduce.5 = (f32[]{:T(128)}, f32[]{:T(128)}) all-reduce(f32[]{:T(128)} %get-tuple-element.238, f32[]{:T(128)} %get-tuple-element.239), channel_id=1, replica_groups=mesh['sx_0'=4,'sx_1'=4,'sy_0'=2,'sy_1'=4,'sy_2'=2] {'sx_1'}, use_global_device_ids=true, to_apply=%region_2.3 | all-reduce | flops 2 | bytes 16 | tf_op jit(solution)/shard_map/psum | solution.py:39
  151.6 8.4 %all-reduce.14 = (f32[]{:T(128)}, f32[]{:T(128)}) all-reduce(f32[]{:T(128)} %get-tuple-element.232, f32[]{:T(128)} %get-tuple-element.233), channel_id=1, replica_groups=mesh['sx_0'=4,'sx_1'=4,'sy_0'=2,'sy_1'=4,'sy_2'=2] {'sy_0'}, use_global_device_ids=true, to_apply=%region_3.4 | all-reduce | flops 2 | bytes 16 | tf_op jit(solution)/shard_map/psum | solution.py:39
  160.0 16.6 %all-reduce.2 = (f32[]{:T(128)}, f32[]{:T(128)}) all-reduce(f32[]{:T(128)} %get-tuple-element.250, f32[]{:T(128)} %get-tuple-element.251), channel_id=1, replica_groups=mesh['sx_0'=4,'sx_1'=4,'sy_0'=2,'sy_1'=4,'sy_2'=2] {'sy_1'}, use_global_device_ids=true, to_apply=%region_4.5 | all-reduce | flops 2 | bytes 16 | tf_op jit(solution)/shard_map/psum | solution.py:39
  176.6 7.7 %all-reduce.11 = (f32[]{:T(128)}, f32[]{:T(128)}) all-reduce(f32[]{:T(128)} %get-tuple-element.226, f32[]{:T(128)} %get-tuple-element.227), channel_id=1, replica_groups=mesh['sx_0'=4,'sx_1'=4,'sy_0'=2,'sy_1'=4,'sy_2'=2] {'sy_2'}, use_global_device_ids=true, to_apply=%region_5.6 | all-reduce | flops 2 | bytes 16 | tf_op jit(solution)/shard_map/psum | solution.py:39
  185.6 5.7 %fusion.41 = f32[1,1024]{1,0:T(1,128)S(1)} fusion(f32[1,1,1024,1024]{3,2,1,0:T(8,128)} %param.40, f32[1,1024]{1,0:T(1,128)S(1)} %bitcast.191, f32[2,1024]{1,0:T(2,128)S(1)} %maximum_add_fusion), kind=kOutput, calls=%fused_computation.63 | convolution fusion | flops 12584960 | bytes 4210688 | tf_op jit(solution)/shard_map/dot_general | solution.py:103
  193.7 5.6 %collective-permute-start.11 = (f32[1,4,128]{2,1,0:T(4,128)S(1)}, f32[1,4,128]{2,1,0:T(4,128)S(1)}, u32[]{:S(2)}, u32[]{:S(2)}) collective-permute-start(f32[1,4,128]{2,1,0:T(4,128)S(1)} %get-tuple-element.273), channel_id=1, source_target_pairs={{16,0},{32,16},{48,32},{64,48},{80,64},{96,80},{112,96},{128,112},... | collective-permute-start | bytes 6152 | tf_op jit(solution)/shard_map/ppermute | solution.py:27
  201.6 4.9 %collective-permute-done.8 = f32[4,1,128]{2,0,1:T(4,128)S(1)} collective-permute-done((f32[4,1,128]{2,0,1:T(4,128)S(1)}, f32[4,1,128]{2,0,1:T(4,128)S(1)}, u32[]{:S(2)}, u32[]{:S(2)}) %collective-permute-start.8) | collective-permute-done | bytes 2080 | tf_op jit(solution)/shard_map/ppermute | solution.py:26
  208.6 6.6 %all-reduce.7 = (f32[]{:T(128)}, f32[]{:T(128)}) all-reduce(f32[]{:T(128)S(6)} %mul.134, f32[]{:T(128)S(6)} %mul.137), channel_id=1, replica_groups=mesh['sx_0'=4,'sx_1'=4,'sy_0'=2,'sy_1'=4,'sy_2'=2] {'sx_0'}, use_global_device_ids=true, to_apply=%region_13.14 | all-reduce | flops 2 | bytes 16 | tf_op jit(solution)/shard_map/psum | solution.py:39
  215.1 7.6 %all-reduce.4 = (f32[]{:T(128)}, f32[]{:T(128)}) all-reduce(f32[]{:T(128)} %get-tuple-element.236, f32[]{:T(128)} %get-tuple-element.237), channel_id=1, replica_groups=mesh['sx_0'=4,'sx_1'=4,'sy_0'=2,'sy_1'=4,'sy_2'=2] {'sx_1'}, use_global_device_ids=true, to_apply=%region_14.15 | all-reduce | flops 2 | bytes 16 | tf_op jit(solution)/shard_map/psum | solution.py:39
  222.7 8.3 %all-reduce.13 = (f32[]{:T(128)}, f32[]{:T(128)}) all-reduce(f32[]{:T(128)} %get-tuple-element.230, f32[]{:T(128)} %get-tuple-element.231), channel_id=1, replica_groups=mesh['sx_0'=4,'sx_1'=4,'sy_0'=2,'sy_1'=4,'sy_2'=2] {'sy_0'}, use_global_device_ids=true, to_apply=%region_15.16 | all-reduce | flops 2 | bytes 16 | tf_op jit(solution)/shard_map/psum | solution.py:39
  231.1 9.7 %all-reduce.1 = (f32[]{:T(128)}, f32[]{:T(128)}) all-reduce(f32[]{:T(128)} %get-tuple-element.248, f32[]{:T(128)} %get-tuple-element.249), channel_id=1, replica_groups=mesh['sx_0'=4,'sx_1'=4,'sy_0'=2,'sy_1'=4,'sy_2'=2] {'sy_1'}, use_global_device_ids=true, to_apply=%region_16.17 | all-reduce | flops 2 | bytes 16 | tf_op jit(solution)/shard_map/psum | solution.py:39
  240.8 14.7 %all-reduce.10 = (f32[]{:T(128)}, f32[]{:T(128)}) all-reduce(f32[]{:T(128)} %get-tuple-element.224, f32[]{:T(128)} %get-tuple-element.225), channel_id=1, replica_groups=mesh['sx_0'=4,'sx_1'=4,'sy_0'=2,'sy_1'=4,'sy_2'=2] {'sy_2'}, use_global_device_ids=true, to_apply=%region_17.18 | all-reduce | flops 2 | bytes 16 | tf_op jit(solution)/shard_map/psum | solution.py:39
  260.1 5.7 %fusion.39 = f32[1,1024]{1,0:T(1,128)S(1)} fusion(f32[1,1024]{1,0:T(1,128)S(1)} %bitcast.188, f32[1,1,1024,1024]{3,2,1,0:T(8,128)} %param.40, f32[1,1024]{1,0:T(1,128)S(1)} %bitcast.192, f32[2,1024]{1,0:T(2,128)S(1)} %maximum_add_fusion), kind=kOutput, calls=%fused_computation.61 | convolution fusion | flops 12585984 | bytes 4214784 | tf_op jit(solution)/shard_map/dot_general | solution.py:103
  269.1 4.3 %collective-permute-start.15 = (f32[1,4,128]{2,1,0:T(4,128)S(1)}, f32[1,4,128]{2,1,0:T(4,128)S(1)}, u32[]{:S(2)}, u32[]{:S(2)}) collective-permute-start(f32[1,4,128]{2,1,0:T(4,128)S(1)} %get-tuple-element.269), channel_id=1, source_target_pairs={{16,0},{32,16},{48,32},{64,48},{80,64},{96,80},{112,96},{128,112},... | collective-permute-start | bytes 6152 | tf_op jit(solution)/shard_map/ppermute | solution.py:27
  279.4 14.4 %all-to-all-start = ((f32[16,1,2304]{2,1,0:T(1,128)}), f32[16,1,2304]{2,1,0:T(1,128)S(1)}, u32[]{:S(2)}, u32[]{:S(2)}) async-start(f32[16,1,2304]{2,1,0:T(1,128)} %reshape.738), calls=%async_computation | async-start | bytes 294912 | tf_op jit(solution)/shard_map/all_to_all | solution.py:50
  295.7 7.1 %all-reduce.6 = (f32[]{:T(128)}, f32[]{:T(128)}) all-reduce(f32[]{:T(128)S(6)} %mul.146, f32[]{:T(128)S(6)} %mul.149), channel_id=1, replica_groups=mesh['sx_0'=4,'sx_1'=4,'sy_0'=2,'sy_1'=4,'sy_2'=2] {'sx_0'}, use_global_device_ids=true, to_apply=%region_25.26 | all-reduce | flops 2 | bytes 16 | tf_op jit(solution)/shard_map/psum | solution.py:39
  302.8 7.2 %all-reduce.3 = (f32[]{:T(128)}, f32[]{:T(128)}) all-reduce(f32[]{:T(128)} %get-tuple-element.234, f32[]{:T(128)} %get-tuple-element.235), channel_id=1, replica_groups=mesh['sx_0'=4,'sx_1'=4,'sy_0'=2,'sy_1'=4,'sy_2'=2] {'sx_1'}, use_global_device_ids=true, to_apply=%region_26.27 | all-reduce | flops 2 | bytes 16 | tf_op jit(solution)/shard_map/psum | solution.py:39
  310.1 8.3 %all-reduce.12 = (f32[]{:T(128)}, f32[]{:T(128)}) all-reduce(f32[]{:T(128)} %get-tuple-element.228, f32[]{:T(128)} %get-tuple-element.229), channel_id=1, replica_groups=mesh['sx_0'=4,'sx_1'=4,'sy_0'=2,'sy_1'=4,'sy_2'=2] {'sy_0'}, use_global_device_ids=true, to_apply=%region_27.28 | all-reduce | flops 2 | bytes 16 | tf_op jit(solution)/shard_map/psum | solution.py:39
  318.4 9.2 %all-reduce = (f32[]{:T(128)}, f32[]{:T(128)}) all-reduce(f32[]{:T(128)} %get-tuple-element.246, f32[]{:T(128)} %get-tuple-element.247), channel_id=1, replica_groups=mesh['sx_0'=4,'sx_1'=4,'sy_0'=2,'sy_1'=4,'sy_2'=2] {'sy_1'}, use_global_device_ids=true, to_apply=%region_28.29 | all-reduce | flops 2 | bytes 16 | tf_op jit(solution)/shard_map/psum | solution.py:39
  327.5 9.7 %all-reduce.9 = (f32[]{:T(128)}, f32[]{:T(128)}) all-reduce(f32[]{:T(128)} %get-tuple-element.222, f32[]{:T(128)} %get-tuple-element.223), channel_id=1, replica_groups=mesh['sx_0'=4,'sx_1'=4,'sy_0'=2,'sy_1'=4,'sy_2'=2] {'sy_2'}, use_global_device_ids=true, to_apply=%region_29.30 | all-reduce | flops 2 | bytes 16 | tf_op jit(solution)/shard_map/psum | solution.py:39
  (140 shorter events, 45.9 us)
Async XLA Ops:
  7.2 89.6 %copy-start = (bf16[1,1,768,1024]{3,2,1,0:T(8,128)(2,1)S(1)}, bf16[1,1,768,1024]{3,2,1,0:T(8,128)(2,1)}, u32[]{:S(2)}) copy-start(bf16[1,1,768,1024]{3,2,1,0:T(8,128)(2,1)} %param.46) | copy-start | bytes 4718596
  7.2 270.1 %reduce-scatter.4.cloned.1.call-start = ((), (), s32[]{:S(2)}) async-start(), calls=%async_computation.2 | async-start | bytes 2506752
  8.1 17.4 %copy-start.1 = (f32[1,1,1024]{2,1,0:T(1,128)S(1)}, f32[1,1,1024]{2,1,0:T(1,128)}, u32[]{:S(2)}) copy-start(f32[1,1,1024]{2,1,0:T(1,128)} %param.41) | copy-start | bytes 12292
  28.1 79.1 %collective-permute-start = (f32[4,1,256]{2,1,0:T(1,128)S(1)}, f32[4,1,256]{2,1,0:T(1,128)S(1)}, u32[]{:S(2)}, u32[]{:S(2)}) collective-permute-start(f32[4,1,256]{2,1,0:T(1,128)S(1)} %get-tuple-element.262), channel_id=1, source_target_pairs={{0,1},{1,2},{2,3},{3,4},{4,5},{5,6},{6,7},{7,8},{8,9},{9,10},{10,1... | collective-permute-start | bytes 12296 | tf_op jit(solution)/shard_map/ppermute | solution.py:26
  30.8 76.4 %collective-permute-start.1 = (f32[4,1,256]{2,1,0:T(1,128)S(1)}, f32[4,1,256]{2,1,0:T(1,128)S(1)}, u32[]{:S(2)}, u32[]{:S(2)}) collective-permute-start(f32[4,1,256]{2,1,0:T(1,128)S(1)} %get-tuple-element.263), channel_id=1, source_target_pairs={{1,0},{2,1},{3,2},{4,3},{5,4},{6,5},{7,6},{8,7},{9,8},{10,9},{11,1... | collective-permute-start | bytes 12296 | tf_op jit(solution)/shard_map/ppermute | solution.py:27
  31.5 75.7 %collective-permute-start.3 = (f32[1,4,256]{2,1,0:T(4,128)S(1)}, f32[1,4,256]{2,1,0:T(4,128)S(1)}, u32[]{:S(2)}, u32[]{:S(2)}) collective-permute-start(f32[1,4,256]{2,1,0:T(4,128)S(1)} %get-tuple-element.265), channel_id=1, source_target_pairs={{16,0},{32,16},{48,32},{64,48},{80,64},{96,80},{112,96},{128,112},... | collective-permute-start | bytes 12296 | tf_op jit(solution)/shard_map/ppermute | solution.py:27
  37.6 69.7 %collective-permute-start.2 = (f32[1,4,256]{2,1,0:T(4,128)S(1)}, f32[1,4,256]{2,1,0:T(4,128)S(1)}, u32[]{:S(2)}, u32[]{:S(2)}) collective-permute-start(f32[1,4,256]{2,1,0:T(4,128)S(1)} %get-tuple-element.264), channel_id=1, source_target_pairs={{0,16},{16,32},{32,48},{48,64},{64,80},{80,96},{96,112},{112,128},... | collective-permute-start | bytes 12296 | tf_op jit(solution)/shard_map/ppermute | solution.py:26
  92.4 1.8 copy-start.2
  115.1 12.7 %collective-permute-start.4 = (f32[4,1,128]{2,1,0:T(1,128)S(1)}, f32[4,1,128]{2,1,0:T(1,128)S(1)}, u32[]{:S(2)}, u32[]{:S(2)}) collective-permute-start(f32[4,1,128]{2,1,0:T(1,128)S(1)} %get-tuple-element.274), channel_id=1, source_target_pairs={{0,1},{1,2},{2,3},{3,4},{4,5},{5,6},{6,7},{7,8},{8,9},{9,10},{10,1... | collective-permute-start | bytes 6152 | tf_op jit(solution)/shard_map/ppermute | solution.py:26
  117.2 10.7 %collective-permute-start.5 = (f32[4,1,128]{2,1,0:T(1,128)S(1)}, f32[4,1,128]{2,1,0:T(1,128)S(1)}, u32[]{:S(2)}, u32[]{:S(2)}) collective-permute-start(f32[4,1,128]{2,1,0:T(1,128)S(1)} %get-tuple-element.275), channel_id=1, source_target_pairs={{1,0},{2,1},{3,2},{4,3},{5,4},{6,5},{7,6},{8,7},{9,8},{10,9},{11,1... | collective-permute-start | bytes 6152 | tf_op jit(solution)/shard_map/ppermute | solution.py:27
  122.2 6.7 %collective-permute-start.6 = (f32[1,4,128]{2,1,0:T(4,128)S(1)}, f32[1,4,128]{2,1,0:T(4,128)S(1)}, u32[]{:S(2)}, u32[]{:S(2)}) collective-permute-start(f32[1,4,128]{2,1,0:T(4,128)S(1)} %get-tuple-element.276), channel_id=1, source_target_pairs={{0,16},{16,32},{32,48},{48,64},{64,80},{80,96},{96,112},{112,128},... | collective-permute-start | bytes 6152 | tf_op jit(solution)/shard_map/ppermute | solution.py:26
  122.2 6.7 %collective-permute-start.7 = (f32[1,4,128]{2,1,0:T(4,128)S(1)}, f32[1,4,128]{2,1,0:T(4,128)S(1)}, u32[]{:S(2)}, u32[]{:S(2)}) collective-permute-start(f32[1,4,128]{2,1,0:T(4,128)S(1)} %get-tuple-element.277), channel_id=1, source_target_pairs={{16,0},{32,16},{48,32},{64,48},{80,64},{96,80},{112,96},{128,112},... | collective-permute-start | bytes 6152 | tf_op jit(solution)/shard_map/ppermute | solution.py:27
  193.2 8.3 %collective-permute-start.9 = (f32[4,1,128]{2,0,1:T(4,128)S(1)}, f32[4,1,128]{2,0,1:T(4,128)S(1)}, u32[]{:S(2)}, u32[]{:S(2)}) collective-permute-start(f32[4,1,128]{2,0,1:T(4,128)S(1)} %bitcast.221), channel_id=1, source_target_pairs={{1,0},{2,1},{3,2},{4,3},{5,4},{6,5},{7,6},{8,7},{9,8},{10,9},{11,1... | collective-permute-start | bytes 6152 | tf_op jit(solution)/shard_map/ppermute | solution.py:27
  193.7 7.9 %collective-permute-start.10 = (f32[1,4,128]{2,1,0:T(4,128)S(1)}, f32[1,4,128]{2,1,0:T(4,128)S(1)}, u32[]{:S(2)}, u32[]{:S(2)}) collective-permute-start(f32[1,4,128]{2,1,0:T(4,128)S(1)} %get-tuple-element.272), channel_id=1, source_target_pairs={{0,16},{16,32},{32,48},{48,64},{64,80},{80,96},{96,112},{112,128},... | collective-permute-start | bytes 6152 | tf_op jit(solution)/shard_map/ppermute | solution.py:26
  193.7 7.9 %collective-permute-start.11 = (f32[1,4,128]{2,1,0:T(4,128)S(1)}, f32[1,4,128]{2,1,0:T(4,128)S(1)}, u32[]{:S(2)}, u32[]{:S(2)}) collective-permute-start(f32[1,4,128]{2,1,0:T(4,128)S(1)} %get-tuple-element.273), channel_id=1, source_target_pairs={{16,0},{32,16},{48,32},{64,48},{80,64},{96,80},{112,96},{128,112},... | collective-permute-start | bytes 6152 | tf_op jit(solution)/shard_map/ppermute | solution.py:27
  199.3 7.2 %collective-permute-start.8 = (f32[4,1,128]{2,0,1:T(4,128)S(1)}, f32[4,1,128]{2,0,1:T(4,128)S(1)}, u32[]{:S(2)}, u32[]{:S(2)}) collective-permute-start(f32[4,1,128]{2,0,1:T(4,128)S(1)} %bitcast.219), channel_id=1, source_target_pairs={{0,1},{1,2},{2,3},{3,4},{4,5},{5,6},{6,7},{7,8},{8,9},{9,10},{10,1... | collective-permute-start | bytes 6152 | tf_op jit(solution)/shard_map/ppermute | solution.py:26
  267.6 8.1 %collective-permute-start.13 = (f32[4,1,128]{2,0,1:T(4,128)S(1)}, f32[4,1,128]{2,0,1:T(4,128)S(1)}, u32[]{:S(2)}, u32[]{:S(2)}) collective-permute-start(f32[4,1,128]{2,0,1:T(4,128)S(1)} %bitcast.222), channel_id=1, source_target_pairs={{1,0},{2,1},{3,2},{4,3},{5,4},{6,5},{7,6},{8,7},{9,8},{10,9},{11,1... | collective-permute-start | bytes 6152 | tf_op jit(solution)/shard_map/ppermute | solution.py:27
  268.1 7.7 %collective-permute-start.14 = (f32[1,4,128]{2,1,0:T(4,128)S(1)}, f32[1,4,128]{2,1,0:T(4,128)S(1)}, u32[]{:S(2)}, u32[]{:S(2)}) collective-permute-start(f32[1,4,128]{2,1,0:T(4,128)S(1)} %get-tuple-element.268), channel_id=1, source_target_pairs={{0,16},{16,32},{32,48},{48,64},{64,80},{80,96},{96,112},{112,128},... | collective-permute-start | bytes 6152 | tf_op jit(solution)/shard_map/ppermute | solution.py:26
  269.1 6.6 %collective-permute-start.15 = (f32[1,4,128]{2,1,0:T(4,128)S(1)}, f32[1,4,128]{2,1,0:T(4,128)S(1)}, u32[]{:S(2)}, u32[]{:S(2)}) collective-permute-start(f32[1,4,128]{2,1,0:T(4,128)S(1)} %get-tuple-element.269), channel_id=1, source_target_pairs={{16,0},{32,16},{48,32},{64,48},{80,64},{96,80},{112,96},{128,112},... | collective-permute-start | bytes 6152 | tf_op jit(solution)/shard_map/ppermute | solution.py:27
  273.4 3.6 %collective-permute-start.12 = (f32[4,1,128]{2,0,1:T(4,128)S(1)}, f32[4,1,128]{2,0,1:T(4,128)S(1)}, u32[]{:S(2)}, u32[]{:S(2)}) collective-permute-start(f32[4,1,128]{2,0,1:T(4,128)S(1)} %bitcast.220), channel_id=1, source_target_pairs={{0,1},{1,2},{2,3},{3,4},{4,5},{5,6},{6,7},{7,8},{8,9},{9,10},{10,1... | collective-permute-start | bytes 6152 | tf_op jit(solution)/shard_map/ppermute | solution.py:26
  279.4 62.4 %all-to-all-start = ((f32[16,1,2304]{2,1,0:T(1,128)}), f32[16,1,2304]{2,1,0:T(1,128)S(1)}, u32[]{:S(2)}, u32[]{:S(2)}) async-start(f32[16,1,2304]{2,1,0:T(1,128)} %reshape.738), calls=%async_computation | async-start | bytes 294912 | tf_op jit(solution)/shard_map/all_to_all | solution.py:50
Sparse Core Ops, SparseCore 0:
  107.2 86.7 reduce-scatter.3
where the time goes:
time: 357 us; the launch traced here: 352 us
  blocking collectives  142 us (40%)
  starting transfers between devices  53.1 us (15%)
  other arithmetic  45.7 us (13%)
  local copies, waits for them, and re-layouts  40.7 us (11%)
  matrix products  34.3 us (10%)
  between operations  28.8 us (8%)
  waiting for transfers between devices  7.27 us (2%)
    psum x15, blocking collectives, by_axis(): return functools.reduce(lax.psum, axes, x)  142 us
    another operation x3, other arithmetic, per_device(): lax.linalg.triangular_solve(chol_interior[0, 0], coupling[0, 0].astype(jn...  40.7 us
    ppermute x8, starting transfers between devices, padded_2(): lax.ppermute(leading, axis, [(b, a) for a, b in up])  28.1 us
    gather x1, local copies, waits for them, and re-layouts, per_device(): jnp.diagonal(local_schur)  17.4 us
    dot_general x3, matrix products, operator(): product = jnp.dot(local_schur, field, precision=lax.Precision.HIGHEST)  17 us
    all_to_all x1, starting transfers between devices, summed_on_arrival(): tiles = lax.all_to_all(cut_along(x, dim, peers), axis, 0, 0, tiled=True)  14.4 us
    ppermute x8, starting transfers between devices, padded_2(): lax.ppermute(last, axis, up)  10.6 us
    another operation x17, local copies, waits for them, and re-layouts  8.99 us
  transfers between devices with their start and end apart: 18, of which 3 were waited for; matrix products, arithmetic and copies ran while one was open for 27% of the time, Pallas kernels for 0%

commit v1 on v0

v1 whole, which is shorter than its diff:
```python
import jax
import jax.numpy as jnp
from jax import lax
from jax.experimental import pallas as pl
from jax.experimental.pallas import tpu as pltpu
from jax.sharding import PartitionSpec as P

F32 = jnp.float32
BF16 = jnp.bfloat16
MESH = pl.DeviceIdType.MESH
NB = 1024
NI = 512
MC = 768
HALF = 384
Q = 96
R = 24


def dims(lhs, rhs):
    return (((lhs,), (rhs,)), ((), ()))


def split(a):
    hi = a.astype(BF16)
    lo = (a - hi.astype(F32)).astype(BF16)
    return hi, lo


def dot(a, b, dn=dims(1, 0)):
    return lax.dot_general(a, b, dn, preferred_element_type=F32)


def dot3(a, b):
    ah, al = split(a)
    bh, bl = split(b)
    return dot(ah, bh) + dot(ah, bl) + dot(al, bh)


def iota(shape, dim):
    return lax.broadcasted_iota(jnp.int32, shape, dim)


def kernel(
    perm,
    bdiag,
    rhs_hbm,
    schur_hbm,
    chol_hbm,
    coup_hbm,
    rest_hbm,
    ext_hbm,
    sol_out,
    res_out,
    next_hbm,
    coarse_out,
    rhs,
    schur,
    chol,
    coup,
    rest,
    ext,
    inv,
    xs,
    follow,
    proj,
    term,
    rawa,
    own,
    sib,
    ring1,
    mid,
    acc2,
    ring2,
    fin,
    last,
    vec,
    send0,
    recv0,
    sendx,
    recvx,
    ar_send,
    ar1,
    ar2,
    load_sem,
    out_sem,
    ex_send,
    ex_recv,
    sib_send,
    sib_recv,
    r1_send,
    r1_recv,
    r2_send,
    r2_recv,
    last_send,
    last_recv,
    a1_send,
    a1_recv,
    a2_send,
    a2_recv,
):
    a = lax.axis_index("sx")
    b = lax.axis_index("sy")
    y, zl = a // 4, a % 4
    zh, x, core = b // 8, (b // 2) % 4, b % 2
    z = zh * 4 + zl

    def device(y_, z_, x_, c_):
        return (y_ * 4 + z_ % 4, (z_ // 4) * 8 + x_ * 2 + c_)

    sibling = device(y, z, x, 1 - core)

    def plane_peer(k):
        return device((y + k // 4) % 4, z, (x + k % 4) % 4, core)

    def column_peer(k):
        return device(y, (z + k // 2) % 8, x, (core + k % 2) % 2)

    neighbours = (
        (a, (b + 15) % 16),
        (a, (b + 1) % 16),
        ((a + 15) % 16, b),
        ((a + 1) % 16, b),
    )

    loads = [
        pltpu.make_async_copy(src, dst, load_sem.at[i])
        for i, (src, dst) in enumerate(
            (
                (rhs_hbm, rhs),
                (chol_hbm, chol),
                (schur_hbm, schur),
                (coup_hbm, coup),
                (ext_hbm, ext),
                (rest_hbm, rest),
            )
        )
    ]
    for load in loads:
        load.start()

    barrier = pltpu.get_barrier_semaphore()

    def greet_plane(k, carry):
        pl.semaphore_signal(barrier, inc=1, device_id=plane_peer(k), device_id_type=MESH)
        return carry

    def greet_column(k, carry):
        pl.semaphore_signal(barrier, inc=1, device_id=column_peer(k), device_id_type=MESH)
        return carry

    for peer in neighbours:
        pl.semaphore_signal(barrier, inc=1, device_id=peer, device_id_type=MESH)
    lax.fori_loop(1, 16, greet_plane, 0)
    lax.fori_loop(1, 16, greet_column, 0)

    row = iota((8, 128), 0)
    swap = jnp.zeros((8, 128), jnp.int32)
    for d in range(4):
        swap = jnp.where(row // 2 == d, perm[d, 0], swap)

    def canonical(v):
        other = jnp.where(row % 2 == 0, pltpu.roll(v, 7, 0), pltpu.roll(v, 1, 0))
        return jnp.where(swap == 1, other, v)

    def from_edges(west, east, south, north):
        low = jnp.where(row < 4, pltpu.roll(west, 6, 0), pltpu.roll(south, 6, 0))
        high = jnp.where(row < 4, pltpu.roll(east, 2, 0), pltpu.roll(north, 2, 0))
        return canonical(jnp.where(row % 4 < 2, low, high))

    def exchange(src, dst, e):
        return [
            pltpu.make_async_remote_copy(
                src_ref=src,
                dst_ref=dst.at[d ^ 1],
                send_sem=ex_send.at[e, d],
                recv_sem=ex_recv.at[e, d ^ 1],
                device_id=neighbours[d],
                device_id_type=MESH,
            )
            for d in range(4)
        ]

    eye = iota((128, 128), 0) == iota((128, 128), 1)

    def matvec(v):
        vec[1] = v

        def body(r, carry):
            rows = pl.ds(pl.multiple_of(r * 128, 128), 128)
            total = jnp.zeros((128, 128), F32)
            for c in range(8):
                total = total + schur[rows, 128 * c : 128 * c + 128] * vec[1, c : c + 1, :]
            vec[0, pl.ds(r, 1), :] = jnp.sum(total.T, axis=0, keepdims=True)
            return carry

        lax.fori_loop(0, 8, body, 0)
        return vec[0]

    loads[0].wait()
    loads[2].wait()

    def diagonal(r, carry):
        at = pl.ds(pl.multiple_of(r * 128, 128), 128)
        vec[0, pl.ds(r, 1), :] = jnp.sum(
            jnp.where(eye, schur[at, at], 0.0), axis=0, keepdims=True
        )
        return carry

    lax.fori_loop(0, 8, diagonal, 0)
    local_rhs = rhs[...]
    local_diag = vec[0]
    send0[0:8, :] = canonical(local_rhs)
    send0[8:16, :] = canonical(local_diag)

    loads[1].wait()
    rr, cc = iota((128, 128), 0), iota((128, 128), 1)

    def invert(t):
        at = pl.ds(pl.multiple_of(t * 128, 128), 128)
        low = chol[at, at]
        on_diag = jnp.where(eye, low, 0.0)
        inv_row = 1.0 / jnp.sum(on_diag, axis=0, keepdims=True)
        inv_col = 1.0 / jnp.sum(on_diag, axis=1, keepdims=True)
        first = (rr == cc + 1) & (rr % 2 == 1)
        got = jnp.where(eye, inv_row, jnp.where(first, -(low * inv_row) * inv_col, 0.0))
        s = 2
        while s < 128:
            part = (rr // (2 * s) == cc // (2 * s)) & ((rr // s) % 2 == 1) & ((cc // s) % 2 == 0)
            got = got - dot3(got, dot3(jnp.where(part, low, 0.0), got))
            s *= 2
        return got

    blocks = [invert(t) for t in range(4)]
    for t in range(4):
        inv[128 * t : 128 * t + 128, 128 * t : 128 * t + 128] = blocks[t]

    pl.semaphore_wait(barrier, 34)
    ex0 = exchange(send0, recv0, 0)
    for copy in ex0:
        copy.start()

    for t in (0, 2):
        inv[128 * t + 128 : 128 * t + 256, 128 * t : 128 * t + 128] = -dot3(
            blocks[t + 1],
            dot3(chol[128 * t + 128 : 128 * t + 256, 128 * t : 128 * t + 128], blocks[t]),
        )
        inv[128 * t : 128 * t + 128, 128 * t + 128 : 128 * t + 256] = jnp.zeros((128, 128), F32)
    inv[256:512, 0:256] = -dot3(
        inv[256:512, 256:512], dot3(chol[256:512, 0:256], inv[0:256, 0:256])
    )

    loads[3].wait()
    top_hi, top_lo = split(inv[0:256, 0:256])
    low_hi, low_lo = split(inv[256:512, :])
    for n in range(0, NB, 256):
        up = coup[0:256, n : n + 256]
        xs[0:256, n : n + 256] = (dot(top_hi, up) + dot(top_lo, up)).astype(BF16)
        full = coup[:, n : n + 256]
        xs[256:512, n : n + 256] = (dot(low_hi, full) + dot(low_lo, full)).astype(BF16)

    def gram(m):
        at = pl.ds(pl.multiple_of(m * 256, 256), 256)
        product = dot(xs[:, at], xs[...], dims(0, 0))
        on = (iota((256, NB), 0) + m * 256) == iota((256, NB), 1)
        follow[at, :] = (jnp.where(on, bdiag[...], 0.0) - product).astype(BF16)

    def gram_range(lo, hi):
        for m in range(lo, hi):
            gram(m)

    for copy in ex0:
        copy.wait()
    assembled_rhs = local_rhs + from_edges(*(recv0[d, 0:8, :] for d in range(4)))
    precond = local_diag + from_edges(*(recv0[d, 8:16, :] for d in range(4)))
    p0 = assembled_rhs
    w0 = p0 / precond
    local0 = matvec(w0)
    sendx[0] = canonical(local0)
    ex1 = exchange(sendx.at[0], recvx.at[0], 1)
    for copy in ex1:
        copy.start()

    gram_range(0, 4)
    store = pltpu.make_async_copy(follow, next_hbm, out_sem)
    store.start()
    loads[4].wait()

    def project(h):
        proj[...] = dot(follow[...], ext[:, HALF * h : HALF * h + HALF]).astype(BF16)

    project(0)

    for copy in ex1:
        copy.wait()
    q0 = local0 + from_edges(*(recvx[0, d] for d in range(4)))
    p1 = q0 - p0
    w1 = p1 / precond
    local1 = matvec(w1)
    sendx[1] = canonical(local1)
    ex2 = exchange(sendx.at[1], recvx.at[1], 2)
    for copy in ex2:
        copy.start()

    loads[5].wait()
    sends_sib = [
        pltpu.make_async_remote_copy(
            src_ref=own.at[1 - core, h],
            dst_ref=sib.at[h],
            send_sem=sib_send.at[h],
            recv_sem=sib_recv.at[h],
            device_id=sibling,
            device_id_type=MESH,
        )
        for h in range(2)
    ]

    def terms(h):
        term[...] = dot(rest[...], proj[...])
        for k in range(16):
            rawa[R * k : R * k + R, :] = term[2 * R * k : 2 * R * k + R, :]
            own[1, h, k // 4, R * (k % 4) : R * (k % 4) + R, :] = term[
                2 * R * k + R : 2 * R * k + 2 * R, :
            ]
        flipped = rawa[...].T
        for u in range(4):
            own[0, h, u] = flipped[Q * u : Q * u + Q, :]
        sends_sib[h].start()

    terms(0)
    project(1)
    terms(1)

    for copy in ex2:
        copy.wait()
    q1 = local1 + from_edges(*(recvx[1, d] for d in range(4)))
    p2 = q1 - p1
    w2 = p2 / precond
    local2 = matvec(w2)
    sendx[2] = canonical(local2)
    ex3 = exchange(sendx.at[2], recvx.at[2], 3)
    for copy in ex3:
        copy.start()

    products = (
        0.5 * w0 * p0,
        0.5 * w0 * p1,
        0.5 * w1 * p1,
        0.5 * w1 * p2,
        0.5 * w2 * p2,
        w2 * local2,
    )
    rows = jnp.zeros((8, 128), F32)
    for i, product in enumerate(products):
        rows = jnp.where(row == i, jnp.sum(product, axis=0, keepdims=True), rows)
    sums = jnp.sum(rows, axis=1, keepdims=True)
    mine = jnp.sum(jnp.where(iota((8, 128), 1) == row, sums, 0.0), axis=0, keepdims=True)
    ar_send[0] = mine

    def gather(stage, k):
        return pltpu.make_async_remote_copy(
            src_ref=ar_send.at[stage],
            dst_ref=(ar1, ar2)[stage].at[k],
            send_sem=(a1_send, a2_send)[stage].at[k],
            recv_sem=(a1_recv, a2_recv)[stage].at[k],
            device_id=(plane_peer, column_peer)[stage](k),
            device_id_type=MESH,
        )

    def gather_start(stage):
        def body(k, carry):
            gather(stage, k).start()
            return carry

        lax.fori_loop(1, 16, body, 0)

    def gather_sum(stage, start):
        def wait(k, carry):
            gather(stage, k).wait()
            return carry

        lax.fori_loop(1, 16, wait, 0)
        total = start
        for k in range(1, 16):
            total = total + (ar1, ar2)[stage][k]
        return total

    gather_start(0)

    def ring(data, bufs, send_sem, recv_sem, along_x):
        here = jnp.where(along_x, x, y)
        right, left, across = (here + 1) % 4, (here + 3) % 4, (here + 2) % 4

        def at(place):
            return device(jnp.where(along_x, y, place), z, jnp.where(along_x, place, x), core)

        def copy(h, slot, chunk, place):
            return pltpu.make_async_remote_copy(
                src_ref=data.at[h, chunk],
                dst_ref=bufs.at[h, slot],
                send_sem=send_sem.at[h, slot],
                recv_sem=recv_sem.at[h, slot],
                device_id=at(place),
                device_id_type=MESH,
            )

        ahead = (right, left)
        behind = (left, right)

        def first(h):
            copy(h, 0, across, ahead[h]).start()
            copy(h, 1, behind[h], behind[h]).start()

        def second(h):
            copy(h, 0, across, ahead[h]).wait()
            data[h, ahead[h]] = data[h, ahead[h]] + bufs[h, 0]
            copy(h, 2, ahead[h], ahead[h]).start()

        def third(h):
            copy(h, 1, behind[h], behind[h]).wait()
            copy(h, 2, ahead[h], ahead[h]).wait()
            return data[h, here] + bufs[h, 1] + bufs[h, 2]

        return first, second, third

    mine_of = own.at[core]
    first1, second1, third1 = ring(mine_of, ring1, r1_send, r1_recv, core == 0)
    for h in range(2):
        sends_sib[h].wait()
        for u in range(4):
            mine_of[h, u] = mine_of[h, u] + sib[h, u]
        first1(h)

    total1 = gather_sum(0, ar_send[0])
    ar_send[1] = total1
    gather_start(1)

    second1(0)
    second1(1)
    first2, second2, third2 = ring(acc2, ring2, r2_send, r2_recv, core == 1)
    for h in range(2):
        mid[0:Q, :] = third1(h)
        mid[Q:128, :] = jnp.zeros((128 - Q, HALF), F32)
        turned = mid[...].T
        for v in range(4):
            acc2[h, v] = turned[Q * v : Q * v + Q, :]
        first2(h)

    moments = gather_sum(1, ar_send[1])
    lane = iota((1, 128), 1)
    g = [
        jnp.sum(jnp.where(lane == i, moments, 0.0), axis=1, keepdims=True) for i in range(6)
    ]
    g[5] = g[5] - g[4]

    def form(u, v, shift):
        total = None
        for i, ui in enumerate(u):
            for j, vj in enumerate(v):
                if ui is None or vj is None:
                    continue
                part = ui * vj * (g[i + j] + g[i + j + 1] if shift else g[i + j])
                total = part if total is None else total + part
        return total

    def plus(u, s, v):
        return [
            p if q is None else (s * q if p is None else p + s * q) for p, q in zip(u, v)
        ]

    one = jnp.ones((1, 1), F32)
    scaled = [one, None, None]
    direction = [one, None, None]
    amount = [None, None, None]
    norm = form(scaled, scaled, False)
    for step in range(3):
        size = norm / form(direction, direction, True)
        amount = plus(amount, size, direction)
        if step < 2:
            image = plus(direction, one, [None] + direction[:2])
            scaled = plus(scaled, -size, image)
            following = form(scaled, scaled, False)
            direction = plus(scaled, following / norm, direction)
            norm = following
    for copy in ex3:
        copy.wait()
    q2 = local2 + from_edges(*(recvx[2, d] for d in range(4)))
    sol_out[...] = amount[0] * w0 + amount[1] * w1 + amount[2] * w2
    res_out[...] = p0 - (amount[0] * q0 + amount[1] * q1 + amount[2] * q2)

    second2(0)
    second2(1)
    for h in range(2):
        mid[0:Q, 0:128] = third2(h)
        got = mid[:, 0:128]
        got = jnp.where(core == 1, got.T, got)
        for k in range(4):
            fin[4 * h + k] = got[R * k : R * k + R, :]

    def spread(k):
        return pltpu.make_async_remote_copy(
            src_ref=fin.at[(z + k // 2) % 8],
            dst_ref=last.at[k],
            send_sem=last_send.at[k],
            recv_sem=last_recv.at[k],
            device_id=column_peer(k),
            device_id_type=MESH,
        )

    def spread_start(k, carry):
        spread(k).start()
        return carry

    def spread_wait(k, carry):
        spread(k).wait()
        return carry

    lax.fori_loop(1, 16, spread_start, 0)
    lax.fori_loop(1, 16, spread_wait, 0)
    same = fin[z]
    for k in range(2, 16, 2):
        same = same + last[k]
    other = last[1]
    for k in range(3, 16, 2):
        other = other + last[k]
    for colour in range(2):
        rows_of = jnp.where(core == colour, same, other)
        rows_of = jnp.where(core == 0, rows_of, pltpu.roll(rows_of, 80, 1))
        coarse_out[R * colour : R * colour + R, :] = rows_of[:, 0:48]
    store.wait()


def per_device(
    schur, rhs_local, edge_perm, chol_interior, coupling, boundary_diag, restrict, extend
):
    any_ = pl.BlockSpec(memory_space=pl.ANY)
    vmem = pl.BlockSpec(memory_space=pltpu.VMEM)
    dma = pltpu.SemaphoreType.DMA
    out = pl.pallas_call(
        kernel,
        out_shape=(
            jax.ShapeDtypeStruct((8, 128), F32),
            jax.ShapeDtypeStruct((8, 128), F32),
            jax.ShapeDtypeStruct((NB, NB), BF16),
            jax.ShapeDtypeStruct((48, 48), F32),
        ),
        in_specs=[pl.BlockSpec(memory_space=pltpu.SMEM), vmem] + [any_] * 6,
        out_specs=(vmem, vmem, any_, vmem),
        scratch_shapes=[
            pltpu.VMEM((8, 128), F32),
            pltpu.VMEM((NB, NB), F32),
            pltpu.VMEM((NI, NI), F32),
            pltpu.VMEM((NI, NB), BF16),
            pltpu.VMEM((MC, NB), BF16),
            pltpu.VMEM((NB, MC), BF16),
            pltpu.VMEM((NI, NI), F32),
            pltpu.VMEM((NI, NB), BF16),
            pltpu.VMEM((NB, NB), BF16),
            pltpu.VMEM((NB, HALF), BF16),
            pltpu.VMEM((MC, HALF), F32),
            pltpu.VMEM((HALF, HALF), F32),
            pltpu.VMEM((2, 2, 4, Q, HALF), F32),
            pltpu.VMEM((2, 4, Q, HALF), F32),
            pltpu.VMEM((2, 3, Q, HALF), F32),
            pltpu.VMEM((128, HALF), F32),
            pltpu.VMEM((2, 4, Q, 128), F32),
            pltpu.VMEM((2, 3, Q, 128), F32),
            pltpu.VMEM((8, R, 128), F32),
            pltpu.VMEM((16, R, 128), F32),
            pltpu.VMEM((2, 8, 128), F32),
            pltpu.VMEM((16, 128), F32),
            pltpu.VMEM((4, 16, 128), F32),
            pltpu.VMEM((3, 8, 128), F32),
            pltpu.VMEM((3, 4, 8, 128), F32),
            pltpu.VMEM((2, 1, 128), F32),
            pltpu.VMEM((16, 1, 128), F32),
            pltpu.VMEM((16, 1, 128), F32),
            dma((6,)),
            dma,
            dma((4, 4)),
            dma((4, 4)),
            dma((2,)),
            dma((2,)),
            dma((2, 3)),
            dma((2, 3)),
            dma((2, 3)),
            dma((2, 3)),
            dma((16,)),
            dma((16,)),
            dma((16,)),
            dma((16,)),
            dma((16,)),
            dma((16,)),
        ],
        compiler_params=pltpu.CompilerParams(
            collective_id=0, has_side_effects=True, vmem_limit_bytes=60 * 1024 * 1024
        ),
        name="interface_and_coarse",
    )(
        edge_perm[0, 0],
        boundary_diag[0],
        rhs_local.reshape(8, 128),
        schur[0, 0],
        chol_interior[0, 0],
        coupling[0, 0],
        restrict[0, 0],
        extend[0, 0],
    )
    sol, res, following, coarse = out
    return sol.reshape(1, 1, NB), res.reshape(1, 1, NB), following[None, None], coarse


def solution(mesh):
    wide = P("sx", "sy", None, None)
    flat = P("sx", "sy", None)
    return jax.shard_map(
        per_device,
        mesh=mesh,
        in_specs=(wide, flat, wide, wide, wide, flat, wide, wide),
        out_specs=(flat, flat, wide, P("sx", "sy")),
        check_vma=False,
    )
```

time: 357 us -> 69.1 us (0.19); the launches traced: 352 us -> 68.9 us
  blocking collectives: 142 us -> 0 us
  Pallas kernels: 0 us -> 60.7 us
  starting transfers between devices: 53.1 us -> 0 us
  other arithmetic: 45.7 us -> 0 us
  matrix products: 34.3 us -> 0 us
  local copies, waits for them, and re-layouts: 40.7 us -> 7.57 us
  between operations: 28.8 us -> 0.64 us
  waiting for transfers between devices: 7.27 us -> 0 us
    psum x15 -> x0, blocking collectives: 142 us -> none  [by_axis(): return functools.reduce(lax.psum, axes, x)]
    pallas_call x0 -> x1, Pallas kernels: none -> 60.7 us  [per_device(): pl.pallas_call(kernel, out_shape=(jax.ShapeDtypeStruct((8, 128), F32), ja...]
    another operation x3 -> x0, other arithmetic: 40.7 us -> none  [per_device(): lax.linalg.triangular_solve(chol_interior[0, 0], coupling[0, 0].astype(jn...]
    ppermute x16 -> x0, starting transfers between devices: 38.7 us -> none  [the longest x8 28.1 us: padded_2(): lax.ppermute(leading, axis, [(b, a) for a, b in up])]
    dot_general x13 -> x0, matrix products: 28.6 us -> none  [the longest x3 17 us: operator(): product = jnp.dot(local_schur, field, precision=lax.Precision.HIGHEST)]
    gather x1 -> x0, local copies, waits for them, and re-layouts: 17.4 us -> none  [per_device(): jnp.diagonal(local_schur)]
    all_to_all x1 -> x0, starting transfers between devices: 14.4 us -> none  [summed_on_arrival(): tiles = lax.all_to_all(cut_along(x, dim, peers), axis, 0, 0, tiled=True)]
    another operation x26 -> x0, local copies, waits for them, and re-layouts: 9.02 us -> none
  transfers between devices with their start and end apart: 18 -> 0, of which waited for: 3 -> 0; matrix products, arithmetic and copies ran while one was open for 27% -> 0% of each run, Pallas kernels for 0% -> 0%
where the time goes in v1:
time: 69.1 us; the launch traced here: 68.9 us
  Pallas kernels  60.7 us (88%)
  local copies, waits for them, and re-layouts  7.57 us (11%)
    pallas_call x1, Pallas kernels, per_device(): pl.pallas_call(kernel, out_shape=(jax.ShapeDtypeStruct((8, 128), F32), ja...  60.7 us
    unnamed x6, local copies, waits for them, and re-layouts  6.24 us

profile of v1, /device:TPU:1, one launch (start us, length us, event | category | flops | bytes accessed | tf_op | source)
XLA Modules:
  0.0 68.9 jit_solution(12584469594597097781)
XLA Ops:
  0.6 1.3 %copy.12.perm = s32[4,2]{1,0:T(4,128)} copy(s32[4,2]{0,1:T(2,128)} %bitcast.21) | data formatting | bytes 64 | tf_op jit(solution)/shard_map/squeeze | solution.py:599
  2.0 60.7 %interface_and_coarse.1 = (f32[8,128]{1,0:T(8,128)}, f32[8,128]{1,0:T(8,128)}, bf16[1024,1024]{1,0:T(8,128)(2,1)}, f32[48,48]{1,0:T(8,128)}) custom-call(s32[4,2]{1,0:T(4,128)} %copy.12.perm, f32[1,1024]{1,0:T(1,128)} %bitcast.17, f32[8,128]{1,0:T(8,128)} %bitcast.18, f32[1024,1024]{1,0:T(8,128)} %bitcast.11, f32[512,512]{1,0:T(8,128)} %bitcast.15, ...), custom_call_target="tpu_custom_call" | custom-call | tf_op jit(solution)/shard_map/interface_and_coarse/pallas_call | solution.py:538
  62.6 1.3 %copy.17 = f32[1,1,1024]{2,1,0:T(1,128)} copy(f32[1,1,1024]{2,1,0:T(1,128)} %bitcast.20) | data formatting | bytes 8192
  63.9 1.3 %copy.18 = f32[1,1,1024]{2,1,0:T(1,128)} copy(f32[1,1,1024]{2,1,0:T(1,128)} %bitcast.19) | data formatting | bytes 8192
  65.2 0.0 copy-start
  65.2 3.1 %copy.19 = bf16[1,1,1024,1024]{3,2,1,0:T(8,128)(2,1)} copy(bf16[1,1,1024,1024]{3,2,1,0:T(8,128)(2,1)} %bitcast.12) | data formatting | bytes 4194304
  68.3 0.0 copy-done
  68.3 0.6 copy.20
Async XLA Ops:
  65.2 3.1 %copy-start = (f32[48,48]{1,0:T(8,128)S(1)}, f32[48,48]{1,0:T(8,128)}, u32[]{:S(2)}) copy-start(f32[48,48]{1,0:T(8,128)} %get-tuple-element.19) | copy-start | bytes 27652

commit v2 on v1

--- a/solution.py
+++ b/solution.py
@@ -36,13 +36,28 @@
     return dot(ah, bh) + dot(ah, bl) + dot(al, bh)
 
 
+def dot3_packed(a, b):
+    ah, al = split(a)
+    bh, bl = split(b)
+    lhs = jnp.concatenate([ah, al], axis=1)
+    rhs = jnp.concatenate(
+        [
+            jnp.concatenate([bh, bl], axis=1),
+            jnp.concatenate([bh, jnp.zeros_like(bl)], axis=1),
+        ],
+        axis=0,
+    )
+    both = dot(lhs, rhs)
+    return both[:, 0:128] + both[:, 128:256]
+
+
 def iota(shape, dim):
     return lax.broadcasted_iota(jnp.int32, shape, dim)
 
 
 def kernel(
-    perm,
-    bdiag,
+    perm_hbm,
+    bdiag_hbm,
     rhs_hbm,
     schur_hbm,
     chol_hbm,
@@ -53,6 +68,8 @@
     res_out,
     next_hbm,
     coarse_out,
+    perm,
+    bdiag,
     rhs,
     schur,
     chol,
@@ -132,11 +149,13 @@
                 (coup_hbm, coup),
                 (ext_hbm, ext),
                 (rest_hbm, rest),
+                (perm_hbm, perm),
+                (bdiag_hbm, bdiag),
             )
         )
     ]
-    for load in loads:
-        load.start()
+    for i in (6, 0, 1, 2, 3, 7, 4, 5):
+        loads[i].start()
 
     barrier = pltpu.get_barrier_semaphore()
 
@@ -154,9 +173,6 @@
     lax.fori_loop(1, 16, greet_column, 0)
 
     row = iota((8, 128), 0)
-    swap = jnp.zeros((8, 128), jnp.int32)
-    for d in range(4):
-        swap = jnp.where(row // 2 == d, perm[d, 0], swap)
 
     def canonical(v):
         other = jnp.where(row % 2 == 0, pltpu.roll(v, 7, 0), pltpu.roll(v, 1, 0))
@@ -196,8 +212,41 @@
         lax.fori_loop(0, 8, body, 0)
         return vec[0]
 
+    rr, cc = iota((128, 128), 0), iota((128, 128), 1)
+    group, place = iota((8, 128), 1) // 8, iota((8, 128), 1) % 8
+
+    def base(t):
+        packed = jnp.zeros((8, 128), F32)
+        for k in range(16):
+            at = 128 * t + 8 * k
+            packed = jnp.where(group == k, chol[at : at + 8, 128 * t : 128 * t + 128], packed)
+        columns = []
+        pivots = jnp.ones((8, 128), F32)
+        for j in range(8):
+            column = jnp.where(place == j, packed, 0.0)
+            if j:
+                column = pltpu.roll(column, 128 - j, 1)
+            for step in (1, 2, 4):
+                column = column + pltpu.roll(column, step, 1)
+            pivots = jnp.where(row == j, column, pivots)
+            columns.append(jnp.where(row > j, column, 0.0))
+        pivots = 1.0 / pivots
+        got = jnp.where(place == row, 1.0, 0.0)
+        for j in range(8):
+            line = got[j : j + 1, :] * pivots[j : j + 1, :]
+            got = jnp.where(row == j, line, got - columns[j] * line)
+        return jnp.concatenate([jnp.where(group == k, got, 0.0) for k in range(16)], axis=0)
+
+    loads[1].wait()
+    blocks = [base(t) for t in range(4)]
+
     loads[0].wait()
     loads[2].wait()
+    loads[6].wait()
+    swap = jnp.zeros((8, 128), jnp.int32)
+    for d in range(4):
+        swap = jnp.where(row // 2 == d, perm[0, d], swap)
+
 
     def diagonal(r, carry):
         at = pl.ds(pl.multiple_of(r * 128, 128), 128)
@@ -212,37 +261,27 @@
     send0[0:8, :] = canonical(local_rhs)
     send0[8:16, :] = canonical(local_diag)
 
-    loads[1].wait()
-    rr, cc = iota((128, 128), 0), iota((128, 128), 1)
-
-    def invert(t):
-        at = pl.ds(pl.multiple_of(t * 128, 128), 128)
-        low = chol[at, at]
-        on_diag = jnp.where(eye, low, 0.0)
-        inv_row = 1.0 / jnp.sum(on_diag, axis=0, keepdims=True)
-        inv_col = 1.0 / jnp.sum(on_diag, axis=1, keepdims=True)
-        first = (rr == cc + 1) & (rr % 2 == 1)
-        got = jnp.where(eye, inv_row, jnp.where(first, -(low * inv_row) * inv_col, 0.0))
-        s = 2
-        while s < 128:
-            part = (rr // (2 * s) == cc // (2 * s)) & ((rr // s) % 2 == 1) & ((cc // s) % 2 == 0)
-            got = got - dot3(got, dot3(jnp.where(part, low, 0.0), got))
-            s *= 2
-        return got
-
-    blocks = [invert(t) for t in range(4)]
-    for t in range(4):
-        inv[128 * t : 128 * t + 128, 128 * t : 128 * t + 128] = blocks[t]
-
     pl.semaphore_wait(barrier, 34)
     ex0 = exchange(send0, recv0, 0)
     for copy in ex0:
         copy.start()
 
+    for s in (8, 16, 32, 64):
+        part = (rr // (2 * s) == cc // (2 * s)) & ((rr // s) % 2 == 1) & ((cc // s) % 2 == 0)
+        inner = [
+            dot3_packed(
+                jnp.where(part, chol[128 * t : 128 * t + 128, 128 * t : 128 * t + 128], 0.0),
+                blocks[t],
+            )
+            for t in range(4)
+        ]
+        blocks = [blocks[t] - dot3_packed(blocks[t], inner[t]) for t in range(4)]
+    for t in range(4):
+        inv[128 * t : 128 * t + 128, 128 * t : 128 * t + 128] = blocks[t]
     for t in (0, 2):
-        inv[128 * t + 128 : 128 * t + 256, 128 * t : 128 * t + 128] = -dot3(
+        inv[128 * t + 128 : 128 * t + 256, 128 * t : 128 * t + 128] = -dot3_packed(
             blocks[t + 1],
-            dot3(chol[128 * t + 128 : 128 * t + 256, 128 * t : 128 * t + 128], blocks[t]),
+            dot3_packed(chol[128 * t + 128 : 128 * t + 256, 128 * t : 128 * t + 128], blocks[t]),
         )
         inv[128 * t : 128 * t + 128, 128 * t + 128 : 128 * t + 256] = jnp.zeros((128, 128), F32)
     inv[256:512, 0:256] = -dot3(
@@ -280,6 +319,7 @@
     for copy in ex1:
         copy.start()
 
+    loads[7].wait()
     gram_range(0, 4)
     store = pltpu.make_async_copy(follow, next_hbm, out_sem)
     store.start()
@@ -287,19 +327,6 @@
 
     def project(h):
         proj[...] = dot(follow[...], ext[:, HALF * h : HALF * h + HALF]).astype(BF16)
-
-    project(0)
-
-    for copy in ex1:
-        copy.wait()
-    q0 = local0 + from_edges(*(recvx[0, d] for d in range(4)))
-    p1 = q0 - p0
-    w1 = p1 / precond
-    local1 = matvec(w1)
-    sendx[1] = canonical(local1)
-    ex2 = exchange(sendx.at[1], recvx.at[1], 2)
-    for copy in ex2:
-        copy.start()
 
     loads[5].wait()
     sends_sib = [
@@ -326,9 +353,123 @@
             own[0, h, u] = flipped[Q * u : Q * u + Q, :]
         sends_sib[h].start()
 
+    place1 = jnp.where(core == 0, x, y)
+    place2 = jnp.where(core == 0, y, x)
+
+    def on_ring(is_x, at):
+        return device(jnp.where(is_x, y, at), z, jnp.where(is_x, at, x), core)
+
+    data = own.at[core]
+    ahead = ((place1 + 1) % 4, (place1 + 3) % 4)
+    behind = ((place1 + 3) % 4, (place1 + 1) % 4)
+    across = (place1 + 2) % 4
+    PART = Q // 2
+
+    def copy1(h, slot):
+        if slot == 4:
+            src, dst, to = data.at[h, behind[h]], ring1.at[h, 2], behind[h]
+        else:
+            chunk = across if slot < 2 else ahead[h]
+            part = pl.ds(PART * (slot % 2), PART)
+            src, dst, to = data.at[h, chunk, part], ring1.at[h, slot // 2, part], ahead[h]
+        return pltpu.make_async_remote_copy(
+            src_ref=src,
+            dst_ref=dst,
+            send_sem=r1_send.at[h, slot],
+            recv_sem=r1_recv.at[h, slot],
+            device_id=on_ring(core == 0, to),
+            device_id_type=MESH,
+        )
+
+    def join(h):
+        sends_sib[h].wait()
+        for u in range(4):
+            data[h, u] = data[h, u] + sib[h, u]
+        copy1(h, 0).start()
+        copy1(h, 1).start()
+
+    def pass_on(h):
+        for i in range(2):
+            part = pl.ds(PART * i, PART)
+            copy1(h, i).wait()
+            data[h, ahead[h], part] = data[h, ahead[h], part] + ring1[h, 0, part]
+            copy1(h, 2 + i).start()
+
+    def copy2(h, k):
+        to = (place2 + k) % 4
+        return pltpu.make_async_remote_copy(
+            src_ref=acc2.at[h, to],
+            dst_ref=ring2.at[h, k - 1],
+            send_sem=r2_send.at[h, k - 1],
+            recv_sem=r2_recv.at[h, k - 1],
+            device_id=on_ring(core == 1, to),
+            device_id_type=MESH,
+        )
+
+    def turn(h):
+        for slot in (2, 3, 4):
+            copy1(h, slot).wait()
+        mid[0:Q, :] = data[h, place1] + ring1[h, 1] + ring1[h, 2]
+        mid[Q:128, :] = jnp.zeros((128 - Q, HALF), F32)
+        turned = mid[...].T
+        for v in range(4):
+            acc2[h, v] = turned[Q * v : Q * v + Q, :]
+        for k in (2, 1, 3):
+            copy2(h, k).start()
+
+    me = z * 2 + core
+
+    def spread(to, source):
+        return pltpu.make_async_remote_copy(
+            src_ref=fin.at[to // 2],
+            dst_ref=last.at[source],
+            send_sem=last_send.at[to],
+            recv_sem=last_recv.at[source],
+            device_id=device(y, to // 2, x, to % 2),
+            device_id_type=MESH,
+        )
+
+    def settle(h):
+        for k in (1, 2, 3):
+            copy2(h, k).wait()
+        mid[0:Q, 0:128] = acc2[h, place2] + ring2[h, 0] + ring2[h, 1] + ring2[h, 2]
+        got = mid[:, 0:128]
+        got = jnp.where(core == 1, got.T, got)
+        for k in range(4):
+            fin[4 * h + k] = got[R * k : R * k + R, :]
+
+        def start(k, carry):
+            @pl.when(k != me)
+            def _():
+                spread(k, me).start()
+
+            return carry
+
+        lax.fori_loop(8 * h, 8 * h + 8, start, 0)
+
+    project(0)
     terms(0)
     project(1)
     terms(1)
+    join(0)
+    copy1(0, 4).start()
+
+    for copy in ex1:
+        copy.wait()
+    q0 = local0 + from_edges(*(recvx[0, d] for d in range(4)))
+    p1 = q0 - p0
+    w1 = p1 / precond
+    local1 = matvec(w1)
+    sendx[1] = canonical(local1)
+    ex2 = exchange(sendx.at[1], recvx.at[1], 2)
+    for copy in ex2:
+        copy.start()
+
+    join(1)
+    pass_on(0)
+    copy1(1, 4).start()
+    pass_on(1)
+    turn(0)
 
     for copy in ex2:
         copy.wait()
@@ -386,64 +527,13 @@
 
     gather_start(0)
 
-    def ring(data, bufs, send_sem, recv_sem, along_x):
-        here = jnp.where(along_x, x, y)
-        right, left, across = (here + 1) % 4, (here + 3) % 4, (here + 2) % 4
-
-        def at(place):
-            return device(jnp.where(along_x, y, place), z, jnp.where(along_x, place, x), core)
-
-        def copy(h, slot, chunk, place):
-            return pltpu.make_async_remote_copy(
-                src_ref=data.at[h, chunk],
-                dst_ref=bufs.at[h, slot],
-                send_sem=send_sem.at[h, slot],
-                recv_sem=recv_sem.at[h, slot],
-                device_id=at(place),
-                device_id_type=MESH,
-            )
-
-        ahead = (right, left)
-        behind = (left, right)
-
-        def first(h):
-            copy(h, 0, across, ahead[h]).start()
-            copy(h, 1, behind[h], behind[h]).start()
-
-        def second(h):
-            copy(h, 0, across, ahead[h]).wait()
-            data[h, ahead[h]] = data[h, ahead[h]] + bufs[h, 0]
-            copy(h, 2, ahead[h], ahead[h]).start()
-
-        def third(h):
-            copy(h, 1, behind[h], behind[h]).wait()
-            copy(h, 2, ahead[h], ahead[h]).wait()
-            return data[h, here] + bufs[h, 1] + bufs[h, 2]
-
-        return first, second, third
-
-    mine_of = own.at[core]
-    first1, second1, third1 = ring(mine_of, ring1, r1_send, r1_recv, core == 0)
-    for h in range(2):
-        sends_sib[h].wait()
-        for u in range(4):
-            mine_of[h, u] = mine_of[h, u] + sib[h, u]
-        first1(h)
-
+    turn(1)
+    settle(0)
     total1 = gather_sum(0, ar_send[0])
     ar_send[1] = total1
     gather_start(1)
-
-    second1(0)
-    second1(1)
-    first2, second2, third2 = ring(acc2, ring2, r2_send, r2_recv, core == 1)
-    for h in range(2):
-        mid[0:Q, :] = third1(h)
-        mid[Q:128, :] = jnp.zeros((128 - Q, HALF), F32)
-        turned = mid[...].T
-        for v in range(4):
-            acc2[h, v] = turned[Q * v : Q * v + Q, :]
-        first2(h)
+    settle(1)
+    last[me] = fin[z]
 
     moments = gather_sum(1, ar_send[1])
     lane = iota((1, 128), 1)
@@ -487,46 +577,41 @@
     sol_out[...] = amount[0] * w0 + amount[1] * w1 + amount[2] * w2
     res_out[...] = p0 - (amount[0] * q0 + amount[1] * q1 + amount[2] * q2)
 
-    second2(0)
-    second2(1)
-    for h in range(2):
-        mid[0:Q, 0:128] = third2(h)
-        got = mid[:, 0:128]
-        got = jnp.where(core == 1, got.T, got)
-        for k in range(4):
-            fin[4 * h + k] = got[R * k : R * k + R, :]
-
-    def spread(k):
-        return pltpu.make_async_remote_copy(
-            src_ref=fin.at[(z + k // 2) % 8],
-            dst_ref=last.at[k],
-            send_sem=last_send.at[k],
-            recv_sem=last_recv.at[k],
-            device_id=column_peer(k),
-            device_id_type=MESH,
-        )
-
-    def spread_start(k, carry):
-        spread(k).start()
+
+    def finish(k, carry):
+        @pl.when(k != me)
+        def _():
+            spread(k, k).wait()
+
         return carry
 
-    def spread_wait(k, carry):
-        spread(k).wait()
-        return carry
-
-    lax.fori_loop(1, 16, spread_start, 0)
-    lax.fori_loop(1, 16, spread_wait, 0)
-    same = fin[z]
-    for k in range(2, 16, 2):
-        same = same + last[k]
-    other = last[1]
-    for k in range(3, 16, 2):
-        other = other + last[k]
+    lax.fori_loop(0, 16, finish, 0)
     for colour in range(2):
-        rows_of = jnp.where(core == colour, same, other)
+        rows_of = last[colour]
+        for k in range(1, 8):
+            rows_of = rows_of + last[2 * k + colour]
         rows_of = jnp.where(core == 0, rows_of, pltpu.roll(rows_of, 80, 1))
         coarse_out[R * colour : R * colour + R, :] = rows_of[:, 0:48]
     store.wait()
+
+
+def store_outputs(
+    sol, res, follow_in, coarse, sol_out, res_out, next_hbm, coarse_out, out_sem
+):
+    part = NB // 4
+    rows = [pl.ds(part * i, part) for i in range(4)]
+    back = [
+        pltpu.make_async_copy(follow_in.at[rows[i]], next_hbm.at[0, 0, rows[i]], out_sem.at[i])
+        for i in range(4)
+    ]
+    for copy in back:
+        copy.start()
+    for k in range(8):
+        sol_out[0, 0:1, 128 * k : 128 * k + 128] = sol[k : k + 1, :]
+        res_out[0, 0:1, 128 * k : 128 * k + 128] = res[k : k + 1, :]
+    coarse_out[...] = coarse[...]
+    for copy in back:
+        copy.wait()
 
 
 def per_device(
@@ -543,9 +628,11 @@
             jax.ShapeDtypeStruct((NB, NB), BF16),
             jax.ShapeDtypeStruct((48, 48), F32),
         ),
-        in_specs=[pl.BlockSpec(memory_space=pltpu.SMEM), vmem] + [any_] * 6,
+        in_specs=[pl.BlockSpec(memory_space=pltpu.HBM)] * 8,
         out_specs=(vmem, vmem, any_, vmem),
         scratch_shapes=[
+            pltpu.SMEM((2, 4), jnp.int32),
+            pltpu.VMEM((1, NB), F32),
             pltpu.VMEM((8, 128), F32),
             pltpu.VMEM((NB, NB), F32),
             pltpu.VMEM((NI, NI), F32),
@@ -574,14 +661,14 @@
             pltpu.VMEM((2, 1, 128), F32),
             pltpu.VMEM((16, 1, 128), F32),
             pltpu.VMEM((16, 1, 128), F32),
-            dma((6,)),
+            dma((8,)),
             dma,
             dma((4, 4)),
             dma((4, 4)),
             dma((2,)),
             dma((2,)),
-            dma((2, 3)),
-            dma((2, 3)),
+            dma((2, 5)),
+            dma((2, 5)),
             dma((2, 3)),
             dma((2, 3)),
             dma((16,)),
@@ -592,21 +679,38 @@
             dma((16,)),
         ],
         compiler_params=pltpu.CompilerParams(
-            collective_id=0, has_side_effects=True, vmem_limit_bytes=60 * 1024 * 1024
+            collective_id=0, has_side_effects=True, vmem_limit_bytes=36 * 1024 * 1024
         ),
         name="interface_and_coarse",
     )(
-        edge_perm[0, 0],
-        boundary_diag[0],
-        rhs_local.reshape(8, 128),
-        schur[0, 0],
-        chol_interior[0, 0],
-        coupling[0, 0],
-        restrict[0, 0],
-        extend[0, 0],
+        *(
+            pltpu.with_memory_space_constraint(array, pltpu.HBM)
+            for array in (
+                edge_perm[0, 0].T,
+                boundary_diag[0],
+                rhs_local.reshape(8, 128),
+                schur[0, 0],
+                chol_interior[0, 0],
+                coupling[0, 0],
+                restrict[0, 0],
+                extend[0, 0],
+            )
+        )
     )
-    sol, res, following, coarse = out
-    return sol.reshape(1, 1, NB), res.reshape(1, 1, NB), following[None, None], coarse
+    return pl.pallas_call(
+        store_outputs,
+        out_shape=(
+            jax.ShapeDtypeStruct((1, 1, NB), F32),
+            jax.ShapeDtypeStruct((1, 1, NB), F32),
+            jax.ShapeDtypeStruct((1, 1, NB, NB), BF16),
+            jax.ShapeDtypeStruct((48, 48), F32),
+        ),
+        in_specs=[vmem, vmem, any_, vmem],
+        out_specs=(vmem, vmem, any_, vmem),
+        scratch_shapes=[dma((4,))],
+        compiler_params=pltpu.CompilerParams(vmem_limit_bytes=4 * 1024 * 1024),
+        name="store_outputs",
+    )(*out)
 
 
 def solution(mesh):

time: 69.1 us -> 47.4 us (0.69)
  Pallas kernels: 60.7 us -> 46.6 us
  local copies, waits for them, and re-layouts: 7.57 us -> 0 us
    pallas_call x1, Pallas kernels: 60.7 us -> 44.7 us  [per_device(): pl.pallas_call(kernel, out_shape=(jax.ShapeDtypeStruct((8, 128), F32), ja...]
    unnamed x6 -> x0, local copies, waits for them, and re-layouts: 6.24 us -> none
    pallas_call x0 -> x1, Pallas kernels: none -> 1.96 us  [per_device(): pl.pallas_call(store_outputs, out_shape=(jax.ShapeDtypeStruct((1, 1, NB),...]
    squeeze x1 -> x0, local copies, waits for them, and re-layouts: 1.34 us -> none  [per_device(): edge_perm[0, 0]]
where the time goes in v2:
time: 47.4 us; the launch traced here: 47.3 us
  Pallas kernels  46.6 us (98%)
  between operations  0.64 us (1%)
    pallas_call x1, Pallas kernels, per_device(): pl.pallas_call(kernel, out_shape=(jax.ShapeDtypeStruct((8, 128), F32), ja...  44.7 us
    pallas_call x1, Pallas kernels, per_device(): pl.pallas_call(store_outputs, out_shape=(jax.ShapeDtypeStruct((1, 1, NB),...  1.96 us

profile of v2, /device:TPU:1, one launch (start us, length us, event | category | flops | bytes accessed | tf_op | source)
XLA Modules:
  0.0 47.3 jit_solution(5936715823018160523)
XLA Ops:
  0.6 44.7 %interface_and_coarse.1 = (f32[8,128]{1,0:T(8,128)S(1)}, f32[8,128]{1,0:T(8,128)S(1)}, bf16[1024,1024]{1,0:T(8,128)(2,1)S(1)}, f32[48,48]{1,0:T(8,128)S(1)}) custom-call(s32[2,4]{1,0:T(2,128)} %bitcast.17, f32[1,1024]{1,0:T(1,128)} %bitcast.15, f32[8,128]{1,0:T(8,128)} %bitcast.16, f32[1024,1024]{1,0:T(8,128)} %bitcast.10, f32[512,512]{1,0:T(8,128)} %bitcast.13, ...), custom_call_target="tpu_custom_call" | custom-call | tf_op jit(solution)/shard_map/interface_and_coarse/pallas_call | solution.py:623
  45.3 2.0 %store_outputs.1 = (f32[1,1,1024]{2,1,0:T(1,128)}, f32[1,1,1024]{2,1,0:T(1,128)}, bf16[1,1,1024,1024]{3,2,1,0:T(8,128)(2,1)}, f32[48,48]{1,0:T(8,128)}) custom-call(f32[8,128]{1,0:T(8,128)S(1)} %get-tuple-element.8.sol, f32[8,128]{1,0:T(8,128)S(1)} %get-tuple-element.9.res, bf16[1024,1024]{1,0:T(8,128)(2,1)S(1)} %get-tuple-element.10.follow_in, ...), custom_call_target="tpu_custom_call" | custom-call | tf_op jit(solution)/shard_map/store_outputs/pallas_call | solution.py:700

commit v3 on v2

--- a/solution.py
+++ b/solution.py
@@ -71,6 +71,7 @@
     perm,
     bdiag,
     rhs,
+    corner,
     schur,
     chol,
     coup,
@@ -80,7 +81,6 @@
     xs,
     follow,
     proj,
-    term,
     rawa,
     own,
     sib,
@@ -91,6 +91,9 @@
     fin,
     last,
     vec,
+    sol,
+    res,
+    coarse,
     send0,
     recv0,
     sendx,
@@ -99,7 +102,9 @@
     ar1,
     ar2,
     load_sem,
+    corner_sem,
     out_sem,
+    result_sem,
     ex_send,
     ex_recv,
     sib_send,
@@ -139,6 +144,13 @@
         ((a + 1) % 16, b),
     )
 
+    barrier = pltpu.get_barrier_semaphore()
+    for peer in neighbours:
+        pl.semaphore_signal(barrier, inc=1, device_id=peer, device_id_type=MESH)
+    for k in range(1, 16):
+        pl.semaphore_signal(barrier, inc=1, device_id=column_peer(k), device_id_type=MESH)
+        pl.semaphore_signal(barrier, inc=1, device_id=plane_peer(k), device_id_type=MESH)
+
     loads = [
         pltpu.make_async_copy(src, dst, load_sem.at[i])
         for i, (src, dst) in enumerate(
@@ -154,23 +166,16 @@
             )
         )
     ]
-    for i in (6, 0, 1, 2, 3, 7, 4, 5):
+    corners = [
+        pltpu.make_async_copy(
+            schur_hbm.at[pl.ds(128 * r, 128), pl.ds(128 * r, 128)], corner.at[r], corner_sem.at[r]
+        )
+        for r in range(8)
+    ]
+    for i in (6, 0, 1):
         loads[i].start()
-
-    barrier = pltpu.get_barrier_semaphore()
-
-    def greet_plane(k, carry):
-        pl.semaphore_signal(barrier, inc=1, device_id=plane_peer(k), device_id_type=MESH)
-        return carry
-
-    def greet_column(k, carry):
-        pl.semaphore_signal(barrier, inc=1, device_id=column_peer(k), device_id_type=MESH)
-        return carry
-
-    for peer in neighbours:
-        pl.semaphore_signal(barrier, inc=1, device_id=peer, device_id_type=MESH)
-    lax.fori_loop(1, 16, greet_plane, 0)
-    lax.fori_loop(1, 16, greet_column, 0)
+    for copy in corners:
+        copy.start()
 
     row = iota((8, 128), 0)
 
@@ -201,15 +206,15 @@
     def matvec(v):
         vec[1] = v
 
-        def body(r, carry):
-            rows = pl.ds(pl.multiple_of(r * 128, 128), 128)
+        for r in range(8):
             total = jnp.zeros((128, 128), F32)
             for c in range(8):
-                total = total + schur[rows, 128 * c : 128 * c + 128] * vec[1, c : c + 1, :]
-            vec[0, pl.ds(r, 1), :] = jnp.sum(total.T, axis=0, keepdims=True)
-            return carry
-
-        lax.fori_loop(0, 8, body, 0)
+                total = (
+                    total
+                    + schur[128 * r : 128 * r + 128, 128 * c : 128 * c + 128]
+                    * vec[1, c : c + 1, :]
+                )
+            vec[0, r : r + 1, :] = jnp.sum(total.T, axis=0, keepdims=True)
         return vec[0]
 
     rr, cc = iota((128, 128), 0), iota((128, 128), 1)
@@ -241,21 +246,18 @@
     blocks = [base(t) for t in range(4)]
 
     loads[0].wait()
-    loads[2].wait()
     loads[6].wait()
     swap = jnp.zeros((8, 128), jnp.int32)
     for d in range(4):
         swap = jnp.where(row // 2 == d, perm[0, d], swap)
 
 
-    def diagonal(r, carry):
-        at = pl.ds(pl.multiple_of(r * 128, 128), 128)
-        vec[0, pl.ds(r, 1), :] = jnp.sum(
-            jnp.where(eye, schur[at, at], 0.0), axis=0, keepdims=True
-        )
-        return carry
-
-    lax.fori_loop(0, 8, diagonal, 0)
+    for copy in corners:
+        copy.wait()
+    for i in (3, 2, 7, 4, 5):
+        loads[i].start()
+    for r in range(8):
+        vec[0, r : r + 1, :] = jnp.sum(jnp.where(eye, corner[r], 0.0), axis=0, keepdims=True)
     local_rhs = rhs[...]
     local_diag = vec[0]
     send0[0:8, :] = canonical(local_rhs)
@@ -307,8 +309,12 @@
         for m in range(lo, hi):
             gram(m)
 
+    loads[7].wait()
+    gram_range(0, 4)
+
     for copy in ex0:
         copy.wait()
+    loads[2].wait()
     assembled_rhs = local_rhs + from_edges(*(recv0[d, 0:8, :] for d in range(4)))
     precond = local_diag + from_edges(*(recv0[d, 8:16, :] for d in range(4)))
     p0 = assembled_rhs
@@ -319,39 +325,42 @@
     for copy in ex1:
         copy.start()
 
-    loads[7].wait()
-    gram_range(0, 4)
     store = pltpu.make_async_copy(follow, next_hbm, out_sem)
     store.start()
     loads[4].wait()
 
+    loads[5].wait()
+    PART = Q // 2
+
+    def to_sibling(h, i):
+        part = pl.ds(PART * i, PART)
+        return pltpu.make_async_remote_copy(
+            src_ref=own.at[1 - core, h, :, part],
+            dst_ref=sib.at[h, :, part],
+            send_sem=sib_send.at[h, i],
+            recv_sem=sib_recv.at[h, i],
+            device_id=sibling,
+            device_id_type=MESH,
+        )
+
     def project(h):
         proj[...] = dot(follow[...], ext[:, HALF * h : HALF * h + HALF]).astype(BF16)
 
-    loads[5].wait()
-    sends_sib = [
-        pltpu.make_async_remote_copy(
-            src_ref=own.at[1 - core, h],
-            dst_ref=sib.at[h],
-            send_sem=sib_send.at[h],
-            recv_sem=sib_recv.at[h],
-            device_id=sibling,
-            device_id_type=MESH,
-        )
-        for h in range(2)
-    ]
-
-    def terms(h):
-        term[...] = dot(rest[...], proj[...])
-        for k in range(16):
-            rawa[R * k : R * k + R, :] = term[2 * R * k : 2 * R * k + R, :]
+    def terms(h, half):
+        term = dot(rest[HALF * half : HALF * half + HALF, :], proj[...])
+        for j in range(8):
+            k = 8 * half + j
+            rawa[R * k : R * k + R, :] = term[2 * R * j : 2 * R * j + R, :]
             own[1, h, k // 4, R * (k % 4) : R * (k % 4) + R, :] = term[
-                2 * R * k + R : 2 * R * k + 2 * R, :
+                2 * R * j + R : 2 * R * j + 2 * R, :
             ]
+
+    def arrange(h):
         flipped = rawa[...].T
         for u in range(4):
             own[0, h, u] = flipped[Q * u : Q * u + Q, :]
-        sends_sib[h].start()
+        to_sibling(h, 0).start()
+        to_sibling(h, 1).start()
 
     place1 = jnp.where(core == 0, x, y)
     place2 = jnp.where(core == 0, y, x)
@@ -363,8 +372,6 @@
     ahead = ((place1 + 1) % 4, (place1 + 3) % 4)
     behind = ((place1 + 3) % 4, (place1 + 1) % 4)
     across = (place1 + 2) % 4
-    PART = Q // 2
-
     def copy1(h, slot):
         if slot == 4:
             src, dst, to = data.at[h, behind[h]], ring1.at[h, 2], behind[h]
@@ -382,11 +389,12 @@
         )
 
     def join(h):
-        sends_sib[h].wait()
-        for u in range(4):
-            data[h, u] = data[h, u] + sib[h, u]
-        copy1(h, 0).start()
-        copy1(h, 1).start()
+        for i in range(2):
+            part = pl.ds(PART * i, PART)
+            to_sibling(h, i).wait()
+            for u in range(4):
+                data[h, u, part] = data[h, u, part] + sib[h, u, part]
+            copy1(h, i).start()
 
     def pass_on(h):
         for i in range(2):
@@ -421,13 +429,15 @@
 
     def spread(to, source):
         return pltpu.make_async_remote_copy(
-            src_ref=fin.at[to // 2],
+            src_ref=fin.at[to],
             dst_ref=last.at[source],
             send_sem=last_send.at[to],
             recv_sem=last_recv.at[source],
             device_id=device(y, to // 2, x, to % 2),
             device_id_type=MESH,
         )
+
+    front = iota((8, 128), 1) < 48
 
     def settle(h):
         for k in (1, 2, 3):
@@ -436,7 +446,12 @@
         got = mid[:, 0:128]
         got = jnp.where(core == 1, got.T, got)
         for k in range(4):
-            fin[4 * h + k] = got[R * k : R * k + R, :]
+            one8, two8, three8 = (got[R * k + 8 * i : R * k + 8 * i + 8, :] for i in range(3))
+            to0, to1 = 8 * h + 2 * k, 8 * h + 2 * k + 1
+            fin[to0, 0:8, :] = jnp.where(front, one8, pltpu.roll(two8, 48, 1))
+            fin[to0, 8:16, :] = three8
+            fin[to1, 0:8, :] = jnp.where(front, pltpu.roll(one8, 80, 1), two8)
+            fin[to1, 8:16, :] = pltpu.roll(three8, 80, 1)
 
         def start(k, carry):
             @pl.when(k != me)
@@ -448,12 +463,15 @@
         lax.fori_loop(8 * h, 8 * h + 8, start, 0)
 
     project(0)
-    terms(0)
+    terms(0, 0)
+    terms(0, 1)
+    arrange(0)
     project(1)
-    terms(1)
+    terms(1, 0)
     join(0)
     copy1(0, 4).start()
-
+    terms(1, 1)
+    arrange(1)
     for copy in ex1:
         copy.wait()
     q0 = local0 + from_edges(*(recvx[0, d] for d in range(4)))
@@ -469,8 +487,6 @@
     pass_on(0)
     copy1(1, 4).start()
     pass_on(1)
-    turn(0)
-
     for copy in ex2:
         copy.wait()
     q1 = local1 + from_edges(*(recvx[1, d] for d in range(4)))
@@ -508,18 +524,12 @@
         )
 
     def gather_start(stage):
-        def body(k, carry):
+        for k in range(1, 16):
             gather(stage, k).start()
-            return carry
-
-        lax.fori_loop(1, 16, body, 0)
 
     def gather_sum(stage, start):
-        def wait(k, carry):
+        for k in range(1, 16):
             gather(stage, k).wait()
-            return carry
-
-        lax.fori_loop(1, 16, wait, 0)
         total = start
         for k in range(1, 16):
             total = total + (ar1, ar2)[stage][k]
@@ -527,13 +537,14 @@
 
     gather_start(0)
 
+    turn(0)
     turn(1)
-    settle(0)
     total1 = gather_sum(0, ar_send[0])
     ar_send[1] = total1
     gather_start(1)
+    settle(0)
     settle(1)
-    last[me] = fin[z]
+    last[me] = fin[me]
 
     moments = gather_sum(1, ar_send[1])
     lane = iota((1, 128), 1)
@@ -574,8 +585,14 @@
     for copy in ex3:
         copy.wait()
     q2 = local2 + from_edges(*(recvx[2, d] for d in range(4)))
-    sol_out[...] = amount[0] * w0 + amount[1] * w1 + amount[2] * w2
-    res_out[...] = p0 - (amount[0] * q0 + amount[1] * q1 + amount[2] * q2)
+    sol[...] = amount[0] * w0 + amount[1] * w1 + amount[2] * w2
+    res[...] = p0 - (amount[0] * q0 + amount[1] * q1 + amount[2] * q2)
+    results = [
+        pltpu.make_async_copy(src, dst, result_sem.at[i])
+        for i, (src, dst) in enumerate(((sol, sol_out), (res, res_out), (coarse, coarse_out)))
+    ]
+    results[0].start()
+    results[1].start()
 
 
     def finish(k, carry):
@@ -590,9 +607,12 @@
         rows_of = last[colour]
         for k in range(1, 8):
             rows_of = rows_of + last[2 * k + colour]
-        rows_of = jnp.where(core == 0, rows_of, pltpu.roll(rows_of, 80, 1))
-        coarse_out[R * colour : R * colour + R, :] = rows_of[:, 0:48]
+        for i, part in enumerate((rows_of[0:8], pltpu.roll(rows_of[0:8], 80, 1), rows_of[8:16])):
+            coarse[R * colour + 8 * i : R * colour + 8 * i + 8, :] = part[:, 0:48]
+    results[2].start()
     store.wait()
+    for copy in results:
+        copy.wait()
 
 
 def store_outputs(
@@ -629,11 +649,12 @@
             jax.ShapeDtypeStruct((48, 48), F32),
         ),
         in_specs=[pl.BlockSpec(memory_space=pltpu.HBM)] * 8,
-        out_specs=(vmem, vmem, any_, vmem),
+        out_specs=(any_,) * 4,
         scratch_shapes=[
             pltpu.SMEM((2, 4), jnp.int32),
             pltpu.VMEM((1, NB), F32),
             pltpu.VMEM((8, 128), F32),
+            pltpu.VMEM((8, 128, 128), F32),
             pltpu.VMEM((NB, NB), F32),
             pltpu.VMEM((NI, NI), F32),
             pltpu.VMEM((NI, NB), BF16),
@@ -643,7 +664,6 @@
             pltpu.VMEM((NI, NB), BF16),
             pltpu.VMEM((NB, NB), BF16),
             pltpu.VMEM((NB, HALF), BF16),
-            pltpu.VMEM((MC, HALF), F32),
             pltpu.VMEM((HALF, HALF), F32),
             pltpu.VMEM((2, 2, 4, Q, HALF), F32),
             pltpu.VMEM((2, 4, Q, HALF), F32),
@@ -651,9 +671,12 @@
             pltpu.VMEM((128, HALF), F32),
             pltpu.VMEM((2, 4, Q, 128), F32),
             pltpu.VMEM((2, 3, Q, 128), F32),
-            pltpu.VMEM((8, R, 128), F32),
-            pltpu.VMEM((16, R, 128), F32),
+            pltpu.VMEM((16, 16, 128), F32),
+            pltpu.VMEM((16, 16, 128), F32),
             pltpu.VMEM((2, 8, 128), F32),
+            pltpu.VMEM((8, 128), F32),
+            pltpu.VMEM((8, 128), F32),
+            pltpu.VMEM((48, 48), F32),
             pltpu.VMEM((16, 128), F32),
             pltpu.VMEM((4, 16, 128), F32),
             pltpu.VMEM((3, 8, 128), F32),
@@ -662,11 +685,13 @@
             pltpu.VMEM((16, 1, 128), F32),
             pltpu.VMEM((16, 1, 128), F32),
             dma((8,)),
+            dma((8,)),
             dma,
+            dma((3,)),
             dma((4, 4)),
             dma((4, 4)),
-            dma((2,)),
-            dma((2,)),
+            dma((2, 2)),
+            dma((2, 2)),
             dma((2, 5)),
             dma((2, 5)),
             dma((2, 3)),

time: 47.4 us -> 42.4 us (0.89)
  Pallas kernels: 46.6 us -> 41.6 us
    pallas_call x1, Pallas kernels: 44.7 us -> 39.6 us  [per_device(): pl.pallas_call(kernel, out_shape=(jax.ShapeDtypeStruct((8, 128), F32), ja...]
where the time goes in v3:
time: 42.4 us; the launch traced here: 42.2 us
  Pallas kernels  41.6 us (98%)
  between operations  0.64 us (2%)
    pallas_call x1, Pallas kernels, per_device(): pl.pallas_call(kernel, out_shape=(jax.ShapeDtypeStruct((8, 128), F32), ja...  39.6 us
    pallas_call x1, Pallas kernels, per_device(): pl.pallas_call(store_outputs, out_shape=(jax.ShapeDtypeStruct((1, 1, NB),...  1.96 us

profile of v3, /device:TPU:1, one launch (start us, length us, event | category | flops | bytes accessed | tf_op | source)
XLA Modules:
  0.0 42.2 jit_solution(2833551457924620475)
XLA Ops:
  0.6 39.6 %interface_and_coarse.1 = (f32[8,128]{1,0:T(8,128)S(1)}, f32[8,128]{1,0:T(8,128)S(1)}, bf16[1024,1024]{1,0:T(8,128)(2,1)S(1)}, f32[48,48]{1,0:T(8,128)S(1)}) custom-call(s32[2,4]{1,0:T(2,128)} %bitcast.17, f32[1,1024]{1,0:T(1,128)} %bitcast.15, f32[8,128]{1,0:T(8,128)} %bitcast.16, f32[1024,1024]{1,0:T(8,128)} %bitcast.10, f32[512,512]{1,0:T(8,128)} %bitcast.13, ...), custom_call_target="tpu_custom_call" | custom-call | tf_op jit(solution)/shard_map/interface_and_coarse/pallas_call | solution.py:643
  40.3 2.0 %store_outputs.1 = (f32[1,1,1024]{2,1,0:T(1,128)}, f32[1,1,1024]{2,1,0:T(1,128)}, bf16[1,1,1024,1024]{3,2,1,0:T(8,128)(2,1)}, f32[48,48]{1,0:T(8,128)}) custom-call(f32[8,128]{1,0:T(8,128)S(1)} %get-tuple-element.8.sol, f32[8,128]{1,0:T(8,128)S(1)} %get-tuple-element.9.res, bf16[1024,1024]{1,0:T(8,128)(2,1)S(1)} %get-tuple-element.10.follow_in, ...), custom_call_target="tpu_custom_call" | custom-call | tf_op jit(solution)/shard_map/store_outputs/pallas_call | solution.py:725
